TPU v7x, 32 devices: a whole 2x2x4 slice. The times are simulated.
32 devices in a mesh: row: 4 (over z), col: 8 (over y, x, core).
Axes of the slice: x: 2, y: 2, z: 4, core: 2. Of those that a mesh axis runs over, the one named last changes fastest.
Arguments:
- v_panels: float32 [8192, 8192], P('row', 'col')
- t_factors: float32 [128, 64, 64], P('col')
- z_vecs: float32 [8192, 1024], P(None, ('row', 'col'))
Outputs:
- output: float32 [8192, 1024], P(None, ('row', 'col'))
All inputs are finite; a program needn't handle non-finite values.
Results may differ from a plain program's by a relative error of at most 0.001.
Values sent between devices are 32-bit elements.
A program may use at most 1 GiB of HBM per device.

v0:
```python
import jax
import jax.numpy as jnp
from jax import lax
from jax.sharding import PartitionSpec as P, NamedSharding

FULL_PREC = lax.Precision.HIGHEST
CONTRACT_ROWS = (((0,), (0,)), ((), ()))


def solution(mesh):
    col_dev = mesh.shape["col"]

    def local_apply(v_loc, t_loc, z_loc):
        num_local = t_loc.shape[0]
        block_w = t_loc.shape[1]
        x_two = lax.all_to_all(z_loc, "row", 0, 1, tiled=True)

        def outer_step(step_idx, x_cur):
            local_idx = num_local - 1 - step_idx
            v_own = lax.dynamic_slice_in_dim(v_loc, local_idx * block_w, block_w, axis=1)
            t_own = lax.dynamic_index_in_dim(t_loc, local_idx, axis=0, keepdims=False)
            v_all = lax.all_gather(v_own, "col")
            t_all = lax.all_gather(t_own, "col")

            def inner_step(sub_idx, x_in):
                owner_col = col_dev - 1 - sub_idx
                v_blk = v_all[owner_col]
                t_blk = t_all[owner_col]
                w_part = lax.dot_general(v_blk, x_in, CONTRACT_ROWS, precision=FULL_PREC, preferred_element_type=jnp.float32)
                w_sum = lax.psum(w_part, "row")
                y_blk = jnp.dot(t_blk, w_sum, precision=FULL_PREC, preferred_element_type=jnp.float32)
                return x_in - jnp.dot(v_blk, y_blk, precision=FULL_PREC, preferred_element_type=jnp.float32)

            return lax.fori_loop(0, col_dev, inner_step, x_cur)

        x_two = lax.fori_loop(0, num_local, outer_step, x_two)
        return lax.all_to_all(x_two, "row", 1, 0, tiled=True)

    return jax.shard_map(
        local_apply,
        mesh=mesh,
        in_specs=(P("row", "col"), P("col", None, None), P(None, ("row", "col"))),
        out_specs=P(None, ("row", "col")),
        check_vma=False,
    )
```

profile of v0, /device:TPU:0, one launch (start us, length us, event | category | flops | bytes accessed | tf_op | source)
XLA Modules:
  0.0 3856.6 jit_solution(15820746038496861699)
XLA Ops:
  41.1 3788.7 %while.44 = (s32[]{:T(128)}, f32[2048,128]{1,0:T(8,128)S(1)}, f32[2048,1024]{1,0:T(8,128)}, f32[16,64,64]{2,1,0:T(8,128)}, s32[]{:T(128)}, /*index=5*/s32[]{:T(1...) while((s32[]{:T(128)}, f32[2048,128]{1,0:T(8,128)S(1)}, ...), condition=%wide.region_4.5_spmd, body=%wide.region_0.4_spmd.sunk | while | flops 409214976 | bytes 25575928 | solution.py:36
  53.8 43.2 %all-gather.5.cloned.1.call-done = f32[16384,64]{1,0:T(8,128)} async-done(((f32[2048,64]{1,0:T(8,128)}), f32[16384,64]{1,0:T(8,128)}) %all-gather.5.cloned.1.call-update) | async-done | bytes 4194320 | tf_op jit(solution)/shard_map/while/body/eval_jaxpr/all_gather | solution.py:22
  97.0 181.7 %while.45 = (s32[]{:T(128)}, f32[2048,128]{1,0:T(8,128)S(1)}, f32[8,2048,64]{2,1,0:T(8,128)}, f32[8,64,64]{2,1,0:T(8,128)S(1)}, s32[]{:T(128)}, /*index=5*/s32[]{:T(128)}, s32[]{:T(128)}, s32[]{:T(128)}) while((s32[]{:T(128)}, f32[2048,128]{1,0:T(8,128)S(1)}, f32[8,2048,64]{2,1,0:T(8,128)}, f32[8,64,64]{2,1,0:T(8,128)S(1)}, s32[]{:T(128)}, ...), condition=%wide.region_3.3_spmd, body=%wide.region_1.2_spmd.sunk | while | flops 409214976 | bytes 5472407 | solution.py:34
  291.7 42.0 %all-gather.5.cloned.1.call-done = f32[16384,64]{1,0:T(8,128)} async-done(((f32[2048,64]{1,0:T(8,128)}), f32[16384,64]{1,0:T(8,128)}) %all-gather.5.cloned.1.call-update) | async-done | bytes 4194320 | tf_op jit(solution)/shard_map/while/body/eval_jaxpr/all_gather | solution.py:22
  333.7 181.7 %while.45 = (s32[]{:T(128)}, f32[2048,128]{1,0:T(8,128)S(1)}, f32[8,2048,64]{2,1,0:T(8,128)}, f32[8,64,64]{2,1,0:T(8,128)S(1)}, s32[]{:T(128)}, /*index=5*/s32[]{:T(128)}, s32[]{:T(128)}, s32[]{:T(128)}) while((s32[]{:T(128)}, f32[2048,128]{1,0:T(8,128)S(1)}, f32[8,2048,64]{2,1,0:T(8,128)}, f32[8,64,64]{2,1,0:T(8,128)S(1)}, s32[]{:T(128)}, ...), condition=%wide.region_3.3_spmd, body=%wide.region_1.2_spmd.sunk | while | flops 409214976 | bytes 5472407 | solution.py:34
  528.5 42.0 %all-gather.5.cloned.1.call-done = f32[16384,64]{1,0:T(8,128)} async-done(((f32[2048,64]{1,0:T(8,128)}), f32[16384,64]{1,0:T(8,128)}) %all-gather.5.cloned.1.call-update) | async-done | bytes 4194320 | tf_op jit(solution)/shard_map/while/body/eval_jaxpr/all_gather | solution.py:22
  570.4 181.7 %while.45 = (s32[]{:T(128)}, f32[2048,128]{1,0:T(8,128)S(1)}, f32[8,2048,64]{2,1,0:T(8,128)}, f32[8,64,64]{2,1,0:T(8,128)S(1)}, s32[]{:T(128)}, /*index=5*/s32[]{:T(128)}, s32[]{:T(128)}, s32[]{:T(128)}) while((s32[]{:T(128)}, f32[2048,128]{1,0:T(8,128)S(1)}, f32[8,2048,64]{2,1,0:T(8,128)}, f32[8,64,64]{2,1,0:T(8,128)S(1)}, s32[]{:T(128)}, ...), condition=%wide.region_3.3_spmd, body=%wide.region_1.2_spmd.sunk | while | flops 409214976 | bytes 5472407 | solution.py:34
  765.2 42.0 %all-gather.5.cloned.1.call-done = f32[16384,64]{1,0:T(8,128)} async-done(((f32[2048,64]{1,0:T(8,128)}), f32[16384,64]{1,0:T(8,128)}) %all-gather.5.cloned.1.call-update) | async-done | bytes 4194320 | tf_op jit(solution)/shard_map/while/body/eval_jaxpr/all_gather | solution.py:22
  807.2 181.7 %while.45 = (s32[]{:T(128)}, f32[2048,128]{1,0:T(8,128)S(1)}, f32[8,2048,64]{2,1,0:T(8,128)}, f32[8,64,64]{2,1,0:T(8,128)S(1)}, s32[]{:T(128)}, /*index=5*/s32[]{:T(128)}, s32[]{:T(128)}, s32[]{:T(128)}) while((s32[]{:T(128)}, f32[2048,128]{1,0:T(8,128)S(1)}, f32[8,2048,64]{2,1,0:T(8,128)}, f32[8,64,64]{2,1,0:T(8,128)S(1)}, s32[]{:T(128)}, ...), condition=%wide.region_3.3_spmd, body=%wide.region_1.2_spmd.sunk | while | flops 409214976 | bytes 5472407 | solution.py:34
  1002.0 42.0 %all-gather.5.cloned.1.call-done = f32[16384,64]{1,0:T(8,128)} async-done(((f32[2048,64]{1,0:T(8,128)}), f32[16384,64]{1,0:T(8,128)}) %all-gather.5.cloned.1.call-update) | async-done | bytes 4194320 | tf_op jit(solution)/shard_map/while/body/eval_jaxpr/all_gather | solution.py:22
  1043.9 181.7 %while.45 = (s32[]{:T(128)}, f32[2048,128]{1,0:T(8,128)S(1)}, f32[8,2048,64]{2,1,0:T(8,128)}, f32[8,64,64]{2,1,0:T(8,128)S(1)}, s32[]{:T(128)}, /*index=5*/s32[]{:T(128)}, s32[]{:T(128)}, s32[]{:T(128)}) while((s32[]{:T(128)}, f32[2048,128]{1,0:T(8,128)S(1)}, f32[8,2048,64]{2,1,0:T(8,128)}, f32[8,64,64]{2,1,0:T(8,128)S(1)}, s32[]{:T(128)}, ...), condition=%wide.region_3.3_spmd, body=%wide.region_1.2_spmd.sunk | while | flops 409214976 | bytes 5472407 | solution.py:34
  1238.7 42.0 %all-gather.5.cloned.1.call-done = f32[16384,64]{1,0:T(8,128)} async-done(((f32[2048,64]{1,0:T(8,128)}), f32[16384,64]{1,0:T(8,128)}) %all-gather.5.cloned.1.call-update) | async-done | bytes 4194320 | tf_op jit(solution)/shard_map/while/body/eval_jaxpr/all_gather | solution.py:22
  1280.7 181.7 %while.45 = (s32[]{:T(128)}, f32[2048,128]{1,0:T(8,128)S(1)}, f32[8,2048,64]{2,1,0:T(8,128)}, f32[8,64,64]{2,1,0:T(8,128)S(1)}, s32[]{:T(128)}, /*index=5*/s32[]{:T(128)}, s32[]{:T(128)}, s32[]{:T(128)}) while((s32[]{:T(128)}, f32[2048,128]{1,0:T(8,128)S(1)}, f32[8,2048,64]{2,1,0:T(8,128)}, f32[8,64,64]{2,1,0:T(8,128)S(1)}, s32[]{:T(128)}, ...), condition=%wide.region_3.3_spmd, body=%wide.region_1.2_spmd.sunk | while | flops 409214976 | bytes 5472407 | solution.py:34
  1475.5 42.0 %all-gather.5.cloned.1.call-done = f32[16384,64]{1,0:T(8,128)} async-done(((f32[2048,64]{1,0:T(8,128)}), f32[16384,64]{1,0:T(8,128)}) %all-gather.5.cloned.1.call-update) | async-done | bytes 4194320 | tf_op jit(solution)/shard_map/while/body/eval_jaxpr/all_gather | solution.py:22
  1517.4 181.7 %while.45 = (s32[]{:T(128)}, f32[2048,128]{1,0:T(8,128)S(1)}, f32[8,2048,64]{2,1,0:T(8,128)}, f32[8,64,64]{2,1,0:T(8,128)S(1)}, s32[]{:T(128)}, /*index=5*/s32[]{:T(128)}, s32[]{:T(128)}, s32[]{:T(128)}) while((s32[]{:T(128)}, f32[2048,128]{1,0:T(8,128)S(1)}, f32[8,2048,64]{2,1,0:T(8,128)}, f32[8,64,64]{2,1,0:T(8,128)S(1)}, s32[]{:T(128)}, ...), condition=%wide.region_3.3_spmd, body=%wide.region_1.2_spmd.sunk | while | flops 409214976 | bytes 5472407 | solution.py:34
  1712.2 42.0 %all-gather.5.cloned.1.call-done = f32[16384,64]{1,0:T(8,128)} async-done(((f32[2048,64]{1,0:T(8,128)}), f32[16384,64]{1,0:T(8,128)}) %all-gather.5.cloned.1.call-update) | async-done | bytes 4194320 | tf_op jit(solution)/shard_map/while/body/eval_jaxpr/all_gather | solution.py:22
  1754.1 181.7 %while.45 = (s32[]{:T(128)}, f32[2048,128]{1,0:T(8,128)S(1)}, f32[8,2048,64]{2,1,0:T(8,128)}, f32[8,64,64]{2,1,0:T(8,128)S(1)}, s32[]{:T(128)}, /*index=5*/s32[]{:T(128)}, s32[]{:T(128)}, s32[]{:T(128)}) while((s32[]{:T(128)}, f32[2048,128]{1,0:T(8,128)S(1)}, f32[8,2048,64]{2,1,0:T(8,128)}, f32[8,64,64]{2,1,0:T(8,128)S(1)}, s32[]{:T(128)}, ...), condition=%wide.region_3.3_spmd, body=%wide.region_1.2_spmd.sunk | while | flops 409214976 | bytes 5472407 | solution.py:34
  1948.9 42.0 %all-gather.5.cloned.1.call-done = f32[16384,64]{1,0:T(8,128)} async-done(((f32[2048,64]{1,0:T(8,128)}), f32[16384,64]{1,0:T(8,128)}) %all-gather.5.cloned.1.call-update) | async-done | bytes 4194320 | tf_op jit(solution)/shard_map/while/body/eval_jaxpr/all_gather | solution.py:22
  1990.9 181.7 %while.45 = (s32[]{:T(128)}, f32[2048,128]{1,0:T(8,128)S(1)}, f32[8,2048,64]{2,1,0:T(8,128)}, f32[8,64,64]{2,1,0:T(8,128)S(1)}, s32[]{:T(128)}, /*index=5*/s32[]{:T(128)}, s32[]{:T(128)}, s32[]{:T(128)}) while((s32[]{:T(128)}, f32[2048,128]{1,0:T(8,128)S(1)}, f32[8,2048,64]{2,1,0:T(8,128)}, f32[8,64,64]{2,1,0:T(8,128)S(1)}, s32[]{:T(128)}, ...), condition=%wide.region_3.3_spmd, body=%wide.region_1.2_spmd.sunk | while | flops 409214976 | bytes 5472407 | solution.py:34
  2185.7 42.0 %all-gather.5.cloned.1.call-done = f32[16384,64]{1,0:T(8,128)} async-done(((f32[2048,64]{1,0:T(8,128)}), f32[16384,64]{1,0:T(8,128)}) %all-gather.5.cloned.1.call-update) | async-done | bytes 4194320 | tf_op jit(solution)/shard_map/while/body/eval_jaxpr/all_gather | solution.py:22
  2227.6 181.7 %while.45 = (s32[]{:T(128)}, f32[2048,128]{1,0:T(8,128)S(1)}, f32[8,2048,64]{2,1,0:T(8,128)}, f32[8,64,64]{2,1,0:T(8,128)S(1)}, s32[]{:T(128)}, /*index=5*/s32[]{:T(128)}, s32[]{:T(128)}, s32[]{:T(128)}) while((s32[]{:T(128)}, f32[2048,128]{1,0:T(8,128)S(1)}, f32[8,2048,64]{2,1,0:T(8,128)}, f32[8,64,64]{2,1,0:T(8,128)S(1)}, s32[]{:T(128)}, ...), condition=%wide.region_3.3_spmd, body=%wide.region_1.2_spmd.sunk | while | flops 409214976 | bytes 5472407 | solution.py:34
  2464.4 181.7 %while.45 = (s32[]{:T(128)}, f32[2048,128]{1,0:T(8,128)S(1)}, f32[8,2048,64]{2,1,0:T(8,128)}, f32[8,64,64]{2,1,0:T(8,128)S(1)}, s32[]{:T(128)}, /*index=5*/s32[]{:T(128)}, s32[]{:T(128)}, s32[]{:T(128)}) while((s32[]{:T(128)}, f32[2048,128]{1,0:T(8,128)S(1)}, f32[8,2048,64]{2,1,0:T(8,128)}, f32[8,64,64]{2,1,0:T(8,128)S(1)}, s32[]{:T(128)}, ...), condition=%wide.region_3.3_spmd, body=%wide.region_1.2_spmd.sunk | while | flops 409214976 | bytes 5472407 | solution.py:34
  2659.2 42.0 %all-gather.5.cloned.1.call-done = f32[16384,64]{1,0:T(8,128)} async-done(((f32[2048,64]{1,0:T(8,128)}), f32[16384,64]{1,0:T(8,128)}) %all-gather.5.cloned.1.call-update) | async-done | bytes 4194320 | tf_op jit(solution)/shard_map/while/body/eval_jaxpr/all_gather | solution.py:22
  2701.1 181.7 %while.45 = (s32[]{:T(128)}, f32[2048,128]{1,0:T(8,128)S(1)}, f32[8,2048,64]{2,1,0:T(8,128)}, f32[8,64,64]{2,1,0:T(8,128)S(1)}, s32[]{:T(128)}, /*index=5*/s32[]{:T(128)}, s32[]{:T(128)}, s32[]{:T(128)}) while((s32[]{:T(128)}, f32[2048,128]{1,0:T(8,128)S(1)}, f32[8,2048,64]{2,1,0:T(8,128)}, f32[8,64,64]{2,1,0:T(8,128)S(1)}, s32[]{:T(128)}, ...), condition=%wide.region_3.3_spmd, body=%wide.region_1.2_spmd.sunk | while | flops 409214976 | bytes 5472407 | solution.py:34
  2895.9 42.0 %all-gather.5.cloned.1.call-done = f32[16384,64]{1,0:T(8,128)} async-done(((f32[2048,64]{1,0:T(8,128)}), f32[16384,64]{1,0:T(8,128)}) %all-gather.5.cloned.1.call-update) | async-done | bytes 4194320 | tf_op jit(solution)/shard_map/while/body/eval_jaxpr/all_gather | solution.py:22
  2937.9 181.7 %while.45 = (s32[]{:T(128)}, f32[2048,128]{1,0:T(8,128)S(1)}, f32[8,2048,64]{2,1,0:T(8,128)}, f32[8,64,64]{2,1,0:T(8,128)S(1)}, s32[]{:T(128)}, /*index=5*/s32[]{:T(128)}, s32[]{:T(128)}, s32[]{:T(128)}) while((s32[]{:T(128)}, f32[2048,128]{1,0:T(8,128)S(1)}, f32[8,2048,64]{2,1,0:T(8,128)}, f32[8,64,64]{2,1,0:T(8,128)S(1)}, s32[]{:T(128)}, ...), condition=%wide.region_3.3_spmd, body=%wide.region_1.2_spmd.sunk | while | flops 409214976 | bytes 5472407 | solution.py:34
  3132.6 42.0 %all-gather.5.cloned.1.call-done = f32[16384,64]{1,0:T(8,128)} async-done(((f32[2048,64]{1,0:T(8,128)}), f32[16384,64]{1,0:T(8,128)}) %all-gather.5.cloned.1.call-update) | async-done | bytes 4194320 | tf_op jit(solution)/shard_map/while/body/eval_jaxpr/all_gather | solution.py:22
  3174.6 181.7 %while.45 = (s32[]{:T(128)}, f32[2048,128]{1,0:T(8,128)S(1)}, f32[8,2048,64]{2,1,0:T(8,128)}, f32[8,64,64]{2,1,0:T(8,128)S(1)}, s32[]{:T(128)}, /*index=5*/s32[]{:T(128)}, s32[]{:T(128)}, s32[]{:T(128)}) while((s32[]{:T(128)}, f32[2048,128]{1,0:T(8,128)S(1)}, f32[8,2048,64]{2,1,0:T(8,128)}, f32[8,64,64]{2,1,0:T(8,128)S(1)}, s32[]{:T(128)}, ...), condition=%wide.region_3.3_spmd, body=%wide.region_1.2_spmd.sunk | while | flops 409214976 | bytes 5472407 | solution.py:34
  3369.4 42.0 %all-gather.5.cloned.1.call-done = f32[16384,64]{1,0:T(8,128)} async-done(((f32[2048,64]{1,0:T(8,128)}), f32[16384,64]{1,0:T(8,128)}) %all-gather.5.cloned.1.call-update) | async-done | bytes 4194320 | tf_op jit(solution)/shard_map/while/body/eval_jaxpr/all_gather | solution.py:22
  3411.3 181.7 %while.45 = (s32[]{:T(128)}, f32[2048,128]{1,0:T(8,128)S(1)}, f32[8,2048,64]{2,1,0:T(8,128)}, f32[8,64,64]{2,1,0:T(8,128)S(1)}, s32[]{:T(128)}, /*index=5*/s32[]{:T(128)}, s32[]{:T(128)}, s32[]{:T(128)}) while((s32[]{:T(128)}, f32[2048,128]{1,0:T(8,128)S(1)}, f32[8,2048,64]{2,1,0:T(8,128)}, f32[8,64,64]{2,1,0:T(8,128)S(1)}, s32[]{:T(128)}, ...), condition=%wide.region_3.3_spmd, body=%wide.region_1.2_spmd.sunk | while | flops 409214976 | bytes 5472407 | solution.py:34
  3606.1 42.0 %all-gather.5.cloned.1.call-done = f32[16384,64]{1,0:T(8,128)} async-done(((f32[2048,64]{1,0:T(8,128)}), f32[16384,64]{1,0:T(8,128)}) %all-gather.5.cloned.1.call-update) | async-done | bytes 4194320 | tf_op jit(solution)/shard_map/while/body/eval_jaxpr/all_gather | solution.py:22
  3648.1 181.7 %while.45 = (s32[]{:T(128)}, f32[2048,128]{1,0:T(8,128)S(1)}, f32[8,2048,64]{2,1,0:T(8,128)}, f32[8,64,64]{2,1,0:T(8,128)S(1)}, s32[]{:T(128)}, /*index=5*/s32[]{:T(128)}, s32[]{:T(128)}, s32[]{:T(128)}) while((s32[]{:T(128)}, f32[2048,128]{1,0:T(8,128)S(1)}, f32[8,2048,64]{2,1,0:T(8,128)}, f32[8,64,64]{2,1,0:T(8,128)S(1)}, s32[]{:T(128)}, ...), condition=%wide.region_3.3_spmd, body=%wide.region_1.2_spmd.sunk | while | flops 409214976 | bytes 5472407 | solution.py:34
  (600 shorter events, 3205.9 us)
Async XLA Ops:
  8.8 31.9 all-to-all-start
  41.1 55.9 %all-gather.5.cloned.1.call-start = ((), (), s32[]{:S(2)}) async-start(), calls=%async_computation.2 | async-start | bytes 9437184 | tf_op jit(solution)/shard_map/while/body/eval_jaxpr/all_gather | solution.py:22
  278.7 55.0 %all-gather.5.cloned.1.call-start = ((), (), s32[]{:S(2)}) async-start(), calls=%async_computation.2 | async-start | bytes 9437184 | tf_op jit(solution)/shard_map/while/body/eval_jaxpr/all_gather | solution.py:22
  515.4 55.0 %all-gather.5.cloned.1.call-start = ((), (), s32[]{:S(2)}) async-start(), calls=%async_computation.2 | async-start | bytes 9437184 | tf_op jit(solution)/shard_map/while/body/eval_jaxpr/all_gather | solution.py:22
  752.1 55.0 %all-gather.5.cloned.1.call-start = ((), (), s32[]{:S(2)}) async-start(), calls=%async_computation.2 | async-start | bytes 9437184 | tf_op jit(solution)/shard_map/while/body/eval_jaxpr/all_gather | solution.py:22
  988.9 55.0 %all-gather.5.cloned.1.call-start = ((), (), s32[]{:S(2)}) async-start(), calls=%async_computation.2 | async-start | bytes 9437184 | tf_op jit(solution)/shard_map/while/body/eval_jaxpr/all_gather | solution.py:22
  1225.6 55.0 %all-gather.5.cloned.1.call-start = ((), (), s32[]{:S(2)}) async-start(), calls=%async_computation.2 | async-start | bytes 9437184 | tf_op jit(solution)/shard_map/while/body/eval_jaxpr/all_gather | solution.py:22
  1462.4 55.0 %all-gather.5.cloned.1.call-start = ((), (), s32[]{:S(2)}) async-start(), calls=%async_computation.2 | async-start | bytes 9437184 | tf_op jit(solution)/shard_map/while/body/eval_jaxpr/all_gather | solution.py:22
  1699.1 55.0 %all-gather.5.cloned.1.call-start = ((), (), s32[]{:S(2)}) async-start(), calls=%async_computation.2 | async-start | bytes 9437184 | tf_op jit(solution)/shard_map/while/body/eval_jaxpr/all_gather | solution.py:22
  1935.8 55.0 %all-gather.5.cloned.1.call-start = ((), (), s32[]{:S(2)}) async-start(), calls=%async_computation.2 | async-start | bytes 9437184 | tf_op jit(solution)/shard_map/while/body/eval_jaxpr/all_gather | solution.py:22
  2172.6 55.0 %all-gather.5.cloned.1.call-start = ((), (), s32[]{:S(2)}) async-start(), calls=%async_computation.2 | async-start | bytes 9437184 | tf_op jit(solution)/shard_map/while/body/eval_jaxpr/all_gather | solution.py:22
  2409.3 55.0 %all-gather.5.cloned.1.call-start = ((), (), s32[]{:S(2)}) async-start(), calls=%async_computation.2 | async-start | bytes 9437184 | tf_op jit(solution)/shard_map/while/body/eval_jaxpr/all_gather | solution.py:22
  2646.1 55.0 %all-gather.5.cloned.1.call-start = ((), (), s32[]{:S(2)}) async-start(), calls=%async_computation.2 | async-start | bytes 9437184 | tf_op jit(solution)/shard_map/while/body/eval_jaxpr/all_gather | solution.py:22
  2882.8 55.0 %all-gather.5.cloned.1.call-start = ((), (), s32[]{:S(2)}) async-start(), calls=%async_computation.2 | async-start | bytes 9437184 | tf_op jit(solution)/shard_map/while/body/eval_jaxpr/all_gather | solution.py:22
  3119.6 55.0 %all-gather.5.cloned.1.call-start = ((), (), s32[]{:S(2)}) async-start(), calls=%async_computation.2 | async-start | bytes 9437184 | tf_op jit(solution)/shard_map/while/body/eval_jaxpr/all_gather | solution.py:22
  3356.3 55.0 %all-gather.5.cloned.1.call-start = ((), (), s32[]{:S(2)}) async-start(), calls=%async_computation.2 | async-start | bytes 9437184 | tf_op jit(solution)/shard_map/while/body/eval_jaxpr/all_gather | solution.py:22
  3593.0 55.0 %all-gather.5.cloned.1.call-start = ((), (), s32[]{:S(2)}) async-start(), calls=%async_computation.2 | async-start | bytes 9437184 | tf_op jit(solution)/shard_map/while/body/eval_jaxpr/all_gather | solution.py:22
Sparse Core Ops, SparseCore 0:
  43.8 53.0 all-gather.4
  281.4 52.2 all-gather.4
  518.1 52.2 all-gather.4
  754.9 52.2 all-gather.4
  991.6 52.2 all-gather.4
  1228.4 52.2 all-gather.4
  1465.1 52.2 all-gather.4
  1701.9 52.2 all-gather.4
  1938.6 52.2 all-gather.4
  2175.3 52.2 all-gather.4
  2412.1 52.2 all-gather.4
  2648.8 52.2 all-gather.4
  2885.6 52.2 all-gather.4
  3122.3 52.2 all-gather.4
  3359.0 52.2 all-gather.4
  3595.8 52.2 all-gather.4
where the time goes:
time: 3870 us; the launch traced here: 3860 us
  blocking collectives  2330 us (60%)
  matrix products  745 us (19%)
  waiting for transfers between devices  698 us (18%)
  local copies, waits for them, and re-layouts  56.9 us (1%)
    psum x128, blocking collectives, inner_step(): w_sum = lax.psum(w_part, 'row')  2160 us
    all_gather x16, waiting for transfers between devices, outer_step(): v_all = lax.all_gather(v_own, 'col')  672 us
    dot_general x128, matrix products, inner_step(): lax.dot_general(v_blk, x_in, CONTRACT_ROWS, precision=FULL_PREC, preferre...  396 us
    dot_general x128, matrix products, inner_step(): jnp.dot(v_blk, y_blk, precision=FULL_PREC, preferred_element_type=jnp.flo...  329 us
    all_gather x16, blocking collectives, outer_step(): t_all = lax.all_gather(t_own, 'col')  155 us
  transfers between devices with their start and end apart: 17, of which 17 were waited for; matrix products, arithmetic and copies ran while one was open for 0% of the time, Pallas kernels for 0%

commit v1 on v0

v1 whole, which is shorter than its diff:
```python
import jax
import jax.numpy as jnp
from jax import lax
from jax.sharding import PartitionSpec as P

HI = lax.Precision.HIGHEST
F32 = jnp.float32


def mm(a, b, ca, cb):
    return lax.dot_general(a, b, (((ca,), (cb,)), ((), ())), precision=HI, preferred_element_type=F32)


def bmm(a, b):
    return jnp.matmul(a, b, precision=HI, preferred_element_type=F32)


def solution(mesh):
    nc = mesh.shape["col"]

    def body(v_loc, t_loc, z_loc):
        nt, bw = t_loc.shape[0], t_loc.shape[1]
        ng = nt // 2
        gw = 2 * bw * nc
        rows = v_loc.shape[0]
        rstep = rows // ng
        x = lax.all_to_all(z_loc, "row", 0, 1, tiled=True)
        t_all = lax.all_gather(t_loc, "col")
        vgs, slabs = {}, []
        for a in range(ng - 1, -1, -1):
            vb = lax.slice(v_loc, (a * rstep, a * 2 * bw), (rows, (a + 1) * 2 * bw))
            vg = lax.all_gather(vb, "col", axis=1, tiled=True)
            vgs[a] = vg
            slabs.append(mm(vg, vb, 0, 0))
        slab = lax.psum(jnp.stack(slabs[::-1]), "row")
        gram = lax.all_gather(slab, "col")
        gram = gram.reshape(nc, ng, nc, 2, bw, 2, bw).transpose(1, 3, 2, 4, 5, 0, 6).reshape(ng, gw, gw)
        cur = t_all.reshape(nc, ng, 2, bw, bw).transpose(1, 2, 0, 3, 4)
        cur = cur.reshape(ng, 2 * nc, bw, bw)
        size, cnt = bw, 2 * nc
        while cnt > 1:
            half = cnt // 2
            g01 = jnp.stack([gram[:, (2 * i) * size:(2 * i + 1) * size, (2 * i + 1) * size:(2 * i + 2) * size]
                             for i in range(half)], axis=1)
            t0, t1 = cur[:, 0::2], cur[:, 1::2]
            t01 = -bmm(t0, bmm(g01, t1))
            top = jnp.concatenate([t0, t01], axis=-1)
            bot = jnp.concatenate([jnp.zeros_like(t01), t1], axis=-1)
            cur = jnp.concatenate([top, bot], axis=-2)
            size, cnt = 2 * size, half
        big = cur[:, 0]
        big = big.reshape(ng, 2, nc, bw, 2, nc, bw).transpose(0, 2, 1, 3, 5, 4, 6).reshape(ng, gw, gw)
        for a in range(ng - 1, -1, -1):
            xs = x[a * rstep:]
            w = lax.psum(mm(vgs[a], xs, 0, 0), "row")
            y = mm(big[a], w, 1, 0)
            xs = xs - mm(vgs[a], y, 1, 0)
            x = jnp.concatenate([x[:a * rstep], xs], axis=0)
        return lax.all_to_all(x, "row", 1, 0, tiled=True)

    return jax.shard_map(
        body,
        mesh=mesh,
        in_specs=(P("row", "col"), P("col", None, None), P(None, ("row", "col"))),
        out_specs=P(None, ("row", "col")),
        check_vma=False,
    )
```

time: 3870 us -> 1660 us (0.43)
  blocking collectives: 2330 us -> 28.3 us
  matrix products: 745 us -> 273 us
  local copies, waits for them, and re-layouts: 56.9 us -> 516 us
  waiting for transfers between devices: 698 us -> 784 us
    psum x128 -> x0, blocking collectives: 2160 us -> none  [inner_step(): w_sum = lax.psum(w_part, 'row')]
    dot_general x384 -> x40, matrix products: 745 us -> 273 us  [the longest x32 212 us: mm(): lax.dot_general(a, b, (((ca,), (cb,)), ((), ())), precision=HI, preferred...]
    psum x0 -> x8, waiting for transfers between devices: none -> 360 us  [the longest x7 189 us: body(): w = lax.psum(mm(vgs[a], xs, 0, 0), 'row')]
    all_gather x16 -> x10, waiting for transfers between devices: 672 us -> 399 us  [the longest x8 207 us: body(): vg = lax.all_gather(vb, 'col', axis=1, tiled=True)]
    reshape x0 -> x4, local copies, waits for them, and re-layouts: none -> 193 us  [the longest x3 190 us: body(): gram.reshape(nc, ng, nc, 2, bw, 2, bw).transpose(1, 3, 2, 4, 5, 0, 6)]
    all_gather x16 -> x0, blocking collectives: 155 us -> none  [outer_step(): t_all = lax.all_gather(t_own, 'col')]
    another operation x0 -> x5, local copies, waits for them, and re-layouts: none -> 146 us  [the longest x2 141 us: body(): big.reshape(ng, 2, nc, bw, 2, nc, bw).transpose(0, 2, 1, 3, 5, 4, 6)]
    squeeze x0 -> x8, local copies, waits for them, and re-layouts: none -> 87.7 us  [body(): y = mm(big[a], w, 1, 0)]
  transfers between devices with their start and end apart: 17 -> 19, of which waited for: 17 -> 18; matrix products, arithmetic and copies ran while one was open for 0% -> 11% of each run, Pallas kernels for 0% -> 0%
where the time goes in v1:
time: 1660 us; the launch traced here: 1650 us
  waiting for transfers between devices  784 us (47%)
  local copies, waits for them, and re-layouts  516 us (31%)
  matrix products  273 us (16%)
  blocking collectives  28.3 us (2%)
  other arithmetic  26.5 us (2%)
    dot_general x32, matrix products, mm(): lax.dot_general(a, b, (((ca,), (cb,)), ((), ())), precision=HI, preferred...  212 us
    all_gather x8, waiting for transfers between devices, body(): vg = lax.all_gather(vb, 'col', axis=1, tiled=True)  207 us
    reshape x3, local copies, waits for them, and re-layouts, body(): gram.reshape(nc, ng, nc, 2, bw, 2, bw).transpose(1, 3, 2, 4, 5, 0, 6)  190 us
    psum x7, waiting for transfers between devices, body(): w = lax.psum(mm(vgs[a], xs, 0, 0), 'row')  189 us
    psum x1, waiting for transfers between devices, body(): slab = lax.psum(jnp.stack(slabs[::-1]), 'row')  170 us
    all_gather x1, waiting for transfers between devices, body(): gram = lax.all_gather(slab, 'col')  156 us
    another operation x2, local copies, waits for them, and re-layouts, body(): big.reshape(ng, 2, nc, bw, 2, nc, bw).transpose(0, 2, 1, 3, 5, 4, 6)  141 us
    squeeze x8, local copies, waits for them, and re-layouts, body(): y = mm(big[a], w, 1, 0)  87.7 us
  transfers between devices with their start and end apart: 19, of which 18 were waited for; matrix products, arithmetic and copies ran while one was open for 11% of the time, Pallas kernels for 0%

profile of v1, /device:TPU:0, one launch (start us, length us, event | category | flops | bytes accessed | tf_op | source)
XLA Modules:
  0.0 1649.6 jit_solution(4644165197400473569)
XLA Ops:
  30.1 23.8 %all-to-all-done = f32[4,2048,32]{1,2,0:T(8,128)S(1)} async-done(((f32[4,2048,32]{1,2,0:T(8,128)}), f32[4,2048,32]{1,2,0:T(8,128)S(1)}, u32[]{:S(2)}, u32[]{:S(2)}) %all-to-all-start) | async-done | bytes 1048608 | tf_op jit(solution)/shard_map/all_to_all | solution.py:27
  58.5 34.1 %all-gather.12.cloned.1.call-done = f32[2048,1024]{1,0:T(8,128)} async-done(((f32[2048,128]{1,0:T(8,128)}), f32[2048,1024]{1,0:T(8,128)}) %all-gather.12.cloned.1.call-update) | async-done | bytes 8388624 | tf_op jit(solution)/shard_map/all_gather | solution.py:32
  92.6 16.5 %fusion.29 = f32[8,1024,128]{2,1,0:T(8,128)} fusion(f32[2048,1024]{1,0:T(8,128)} %all-gather.12.cloned.1.call-done, f32[2048,1024]{1,0:T(8,128)} %param.3), kind=kOutput, calls=%fused_computation.60 | convolution fusion | flops 3221225472 | bytes 9961472 | tf_op jit(solution)/shard_map/dot_general | solution.py:11
  109.2 36.3 %all-gather.14.cloned.1.call-done = f32[1792,1024]{1,0:T(8,128)} async-done(((f32[1792,128]{1,0:T(8,128)}), f32[1792,1024]{1,0:T(8,128)}) %all-gather.14.cloned.1.call-update) | async-done | bytes 7340048 | tf_op jit(solution)/shard_map/all_gather | solution.py:32
  145.4 15.1 fusion.28
  160.6 32.9 %all-gather.16.cloned.1.call-done = f32[1536,1024]{1,0:T(8,128)} async-done(((f32[1536,128]{1,0:T(8,128)}), f32[1536,1024]{1,0:T(8,128)}) %all-gather.16.cloned.1.call-update) | async-done | bytes 6291472 | tf_op jit(solution)/shard_map/all_gather | solution.py:32
  193.5 13.0 fusion.27
  206.5 30.4 %all-gather.18.cloned.1.call-done = f32[1280,1024]{1,0:T(8,128)} async-done(((f32[1280,128]{1,0:T(8,128)}), f32[1280,1024]{1,0:T(8,128)}) %all-gather.18.cloned.1.call-update) | async-done | bytes 5242896 | tf_op jit(solution)/shard_map/all_gather | solution.py:32
  236.9 11.7 fusion.23
  248.6 27.1 %all-gather.20.cloned.1.call-done = f32[1024,1024]{1,0:T(8,128)} async-done(((f32[1024,128]{1,0:T(8,128)}), f32[1024,1024]{1,0:T(8,128)}) %all-gather.20.cloned.1.call-update) | async-done | bytes 4194320 | tf_op jit(solution)/shard_map/all_gather | solution.py:32
  285.9 24.2 %all-gather.22.cloned.1.call-done = f32[768,1024]{1,0:T(8,128)} async-done(((f32[768,128]{1,0:T(8,128)}), f32[768,1024]{1,0:T(8,128)}) %all-gather.22.cloned.1.call-update) | async-done | bytes 3145744 | tf_op jit(solution)/shard_map/all_gather | solution.py:32
  317.8 22.0 %all-gather.24.cloned.1.call-done = f32[512,1024]{1,0:T(8,128)} async-done(((f32[512,128]{1,0:T(8,128)}), f32[512,1024]{1,0:T(8,128)}) %all-gather.24.cloned.1.call-update) | async-done | bytes 2097168 | tf_op jit(solution)/shard_map/all_gather | solution.py:32
  349.8 170.4 %all-reduce.28.cloned.1.call-done = (f32[1,8,1024,128]{3,2,1,0:T(8,128)}, f32[1024,128]{1,0:T(8,128)}) async-done(((f32[1,8,1024,128]{3,2,1,0:T(8,128)}, f32[1024,128]{1,0:T(8,128)}), (f32[1,8,1024,128]{3,2,1,0:T(8,128)}, f32[1024,128]{1,0:T(8,128)})) %all-reduce.28.cloned.1.call-update) | async-done | bytes 4718608 | tf_op jit(solution)/shard_map/psum | solution.py:35
  521.3 36.0 %all-gather.30.cloned.1.call-done = f32[128,64,64]{2,1,0:T(8,128)} async-done(((f32[16,64,64]{2,1,0:T(8,128)}), f32[128,64,64]{2,1,0:T(8,128)}) %all-gather.30.cloned.1.call-update) | async-done | bytes 2097168 | tf_op jit(solution)/shard_map/all_gather | solution.py:28
  563.6 156.4 %all-gather.28.cloned.1.call-done = f32[8,8,1024,128]{3,2,1,0:T(8,128)} async-done(((f32[1,8,1024,128]{3,2,1,0:T(8,128)}), f32[8,8,1024,128]{3,2,1,0:T(8,128)}) %all-gather.28.cloned.1.call-update) | async-done | bytes 33554448 | tf_op jit(solution)/shard_map/all_gather | solution.py:36
  720.0 63.2 %reshape.46 = f32[8,8,8,2,64,2,64]{6,5,4,3,2,1,0:T(2,128)} reshape(f32[8,8,1024,128]{3,2,1,0:T(8,128)} %all-gather.28.cloned.1.call-done) | data formatting | bytes 67108864 | tf_op jit(solution)/shard_map/reshape | solution.py:37
  783.1 71.4 %copy.41 = f32[8,8,8,2,64,2,64]{6,0,5,4,2,3,1:T(8,128)} copy(f32[8,8,8,2,64,2,64]{6,5,4,3,2,1,0:T(2,128)} %reshape.46) | data formatting | bytes 67108864 | tf_op jit(solution)/shard_map/reshape | solution.py:37
  854.5 55.5 %reshape.47 = f32[8,1024,1024]{2,1,0:T(8,128)} reshape(f32[8,2,8,64,2,8,64]{6,5,4,3,2,1,0:T(8,128)} %bitcast.221) | data formatting | bytes 67108864 | tf_op jit(solution)/shard_map/reshape | solution.py:37
  958.3 17.8 %fusion = f32[8,512,512]{1,2,0:T(8,128)} fusion(f32[8,1024,1024]{2,1,0:T(8,128)} %reshape.47, f32[8,2,512,512]{3,2,1,0:T(8,128)S(1)} %select_maximum_fusion.1), kind=kOutput, calls=%fused_computation.6 | convolution fusion | flops 12884901888 | bytes 25165824 | tf_op jit(solution)/shard_map/dot_general | solution.py:15
  982.9 17.1 %negate_bitcast_fusion = f32[8,1,512,512]{3,2,1,0:T(8,128)} fusion(f32[8,512,512]{1,2,0:T(8,128)} %fusion, f32[8,2,512,512]{3,2,1,0:T(8,128)S(1)} %select_maximum_fusion.1), kind=kOutput, calls=%fused_computation.13 | convolution fusion | flops 12886999040 | bytes 25165824 | tf_op jit(solution)/shard_map/dot_general | solution.py:15
  1000.0 20.4 %select_maximum_fusion = f32[8,1,1024,1024]{3,2,1,0:T(8,128)} fusion(f32[8,1,512,512]{3,2,1,0:T(8,128)} %get-tuple-element.22, f32[8,1,512,512]{3,2,1,0:T(8,128)} %negate_bitcast_fusion, f32[8,1,512,512]{3,2,1,0:T(8,128)} %get-tuple-element.21), kind=kLoop, calls=%fused_computation.2 | loop fusion | flops 33554432 | bytes 58720256 | tf_op jit(solution)/shard_map/concatenate | solution.py:49
  1020.4 50.2 %reshape_squeeze.3 = f32[8,2,8,64,2,8,64]{6,5,4,3,2,1,0:T(8,128)} reshape(f32[8,1,1024,1024]{3,2,1,0:T(8,128)} %select_maximum_fusion) | data formatting | bytes 67108864 | tf_op jit(solution)/shard_map/reshape;squeeze | solution.py:52
  1070.6 90.7 %copy.40 = f32[8,2,8,64,2,8,64]{6,4,5,3,1,2,0:T(2,128)} copy(f32[8,2,8,64,2,8,64]{6,5,4,3,2,1,0:T(8,128)} %reshape_squeeze.3) | data formatting | bytes 67108864 | tf_op jit(solution)/shard_map/reshape;squeeze | solution.py:52
  1161.3 44.4 %fusion.67 = (f32[1,8,2,64,8,2,64]{6,5,4,3,2,1,0:T(2,128)}, f32[1,8,2,64,8,2,64]{6,5,4,3,2,1,0:T(2,128)}, f32[1,8,2,64,8,2,64]{6,5,4,3,2,1,0:T(2,128)}, f32[1,8,...) fusion(f32[8,8,2,64,8,2,64]{6,5,4,3,2,1,0:T(2,128)} %bitcast.220), kind=kLoop, calls=%fused_computation.124 | loop fusion | bytes 67108864 | tf_op jit(solution)/shard_map/slice | solution.py:56
  1237.9 26.7 %all-reduce.14.cloned.1.call-done = f32[1024,128]{0,1:T(8,128)} async-done(((f32[1024,128]{0,1:T(8,128)}), f32[1024,128]{0,1:T(8,128)}) %all-reduce.14.cloned.1.call-update) | async-done | bytes 524304 | tf_op jit(solution)/shard_map/psum | solution.py:55
  1289.0 25.5 %all-reduce.16.cloned.1.call-done = f32[1024,128]{0,1:T(8,128)} async-done(((f32[1024,128]{0,1:T(8,128)}), f32[1024,128]{0,1:T(8,128)}) %all-reduce.16.cloned.1.call-update) | async-done | bytes 524304 | tf_op jit(solution)/shard_map/psum | solution.py:55
  1337.9 27.4 %all-reduce.18.cloned.1.call-done = f32[1024,128]{0,1:T(8,128)} async-done(((f32[1024,128]{0,1:T(8,128)}), f32[1024,128]{0,1:T(8,128)}) %all-reduce.18.cloned.1.call-update) | async-done | bytes 524304 | tf_op jit(solution)/shard_map/psum | solution.py:55
  1392.9 27.2 %all-reduce.20.cloned.1.call-done = f32[1024,128]{0,1:T(8,128)} async-done(((f32[1024,128]{0,1:T(8,128)}), f32[1024,128]{0,1:T(8,128)}) %all-reduce.20.cloned.1.call-update) | async-done | bytes 524304 | tf_op jit(solution)/shard_map/psum | solution.py:55
  1450.7 27.5 %all-reduce.22.cloned.1.call-done = f32[1024,128]{0,1:T(8,128)} async-done(((f32[1024,128]{0,1:T(8,128)}), f32[1024,128]{0,1:T(8,128)}) %all-reduce.22.cloned.1.call-update) | async-done | bytes 524304 | tf_op jit(solution)/shard_map/psum | solution.py:55
  1507.1 27.6 %all-reduce.24.cloned.1.call-done = f32[1024,128]{0,1:T(8,128)} async-done(((f32[1024,128]{0,1:T(8,128)}), f32[1024,128]{0,1:T(8,128)}) %all-reduce.24.cloned.1.call-update) | async-done | bytes 524304 | tf_op jit(solution)/shard_map/psum | solution.py:55
  1568.7 27.5 %all-reduce.26.cloned.1.call-done = f32[1024,128]{0,1:T(8,128)} async-done(((f32[1024,128]{0,1:T(8,128)}), f32[1024,128]{0,1:T(8,128)}) %all-reduce.26.cloned.1.call-update) | async-done | bytes 524304 | tf_op jit(solution)/shard_map/psum | solution.py:55
  1613.0 28.3 %all_to_all.35 = f32[2048,4,32]{0,2,1:T(8,128)S(1)} all-to-all(f32[2048,4,32]{0,2,1:T(8,128)S(1)} %bitcast.244), channel_id=1, replica_groups=mesh['row'=4,'col'=8] {'row'}, dimensions={1} | all-to-all | bytes 2097152 | tf_op jit(solution)/shard_map/all_to_all | solution.py:59
  (177 shorter events, 336.4 us)
Async XLA Ops:
  6.5 48.0 %all-gather.26.cloned.1.call-start = ((), (), s32[]{:S(2)}) async-start(), calls=%async_computation.9 | async-start | bytes 1179648 | tf_op jit(solution)/shard_map/all_gather | solution.py:32
  8.1 84.5 %all-gather.12.cloned.1.call-start = ((), (), s32[]{:S(2)}) async-start(), calls=%async_computation.2 | async-start | bytes 9437184 | tf_op jit(solution)/shard_map/all_gather | solution.py:32
  10.5 135.0 %all-gather.14.cloned.1.call-start = ((), (), s32[]{:S(2)}) async-start(), calls=%async_computation.3 | async-start | bytes 8257536 | tf_op jit(solution)/shard_map/all_gather | solution.py:32
  12.8 180.7 %all-gather.16.cloned.1.call-start = ((), (), s32[]{:S(2)}) async-start(), calls=%async_computation.4 | async-start | bytes 7077888 | tf_op jit(solution)/shard_map/all_gather | solution.py:32
  15.0 221.9 %all-gather.18.cloned.1.call-start = ((), (), s32[]{:S(2)}) async-start(), calls=%async_computation.5 | async-start | bytes 5898240 | tf_op jit(solution)/shard_map/all_gather | solution.py:32
  17.1 258.7 %all-gather.20.cloned.1.call-start = ((), (), s32[]{:S(2)}) async-start(), calls=%async_computation.6 | async-start | bytes 4718592 | tf_op jit(solution)/shard_map/all_gather | solution.py:32
  19.0 291.1 %all-gather.22.cloned.1.call-start = ((), (), s32[]{:S(2)}) async-start(), calls=%async_computation.7 | async-start | bytes 3538944 | tf_op jit(solution)/shard_map/all_gather | solution.py:32
  21.9 31.9 %all-to-all-start = ((f32[4,2048,32]{1,2,0:T(8,128)}), f32[4,2048,32]{1,2,0:T(8,128)S(1)}, u32[]{:S(2)}, u32[]{:S(2)}) async-start(f32[4,2048,32]{1,2,0:T(8,128)} %bitcast.222), calls=%async_computation | async-start | bytes 2097152 | tf_op jit(solution)/shard_map/all_to_all | solution.py:27
  28.3 311.5 %all-gather.24.cloned.1.call-start = ((), (), s32[]{:S(2)}) async-start(), calls=%async_computation.8 | async-start | bytes 2359296 | tf_op jit(solution)/shard_map/all_gather | solution.py:32
  30.0 490.2 %all-reduce.28.cloned.1.call-start = ((), (), s32[]{:S(2)}) async-start(), calls=%async_computation.19 | async-start | bytes 9437184 | tf_op jit(solution)/shard_map/psum | solution.py:35
  53.8 466.4 %copy-start.5 = (f32[4,2048,32]{1,2,0:T(8,128)}, f32[4,2048,32]{1,2,0:T(8,128)S(1)}, u32[]{:S(2)}) copy-start(f32[4,2048,32]{1,2,0:T(8,128)S(1)} %all-to-all-done) | copy-start | bytes 3145732
  54.6 54.6 %copy-start.24 = (f32[256,4,32]{0,2,1:T(8,128)}, f32[256,4,32]{0,2,1:T(8,128)S(1)}, u32[]{:S(2)}) copy-start(f32[256,4,32]{0,2,1:T(8,128)S(1)} %get-tuple-element.30) | copy-start | bytes 393220
  285.9 59.7 %copy-start.10 = (f32[256,1024]{1,0:T(8,128)S(1)}, f32[256,1024]{1,0:T(8,128)}, u32[]{:S(2)}) copy-start(f32[256,1024]{1,0:T(8,128)} %all-gather.26.cloned.1.call-done) | copy-start | bytes 3145732
  349.2 208.1 %all-gather.30.cloned.1.call-start = ((), (), s32[]{:S(2)}) async-start(), calls=%async_computation.18 | async-start | bytes 4718592 | tf_op jit(solution)/shard_map/all_gather | solution.py:28
  349.8 370.2 %all-gather.28.cloned.1.call-start = ((), (), s32[]{:S(2)}) async-start(), calls=%async_computation.10 | async-start | bytes 37748736 | tf_op jit(solution)/shard_map/all_gather | solution.py:36
  520.2 744.4 %all-reduce.14.cloned.1.call-start = ((), (), s32[]{:S(2)}) async-start(), calls=%async_computation.11 | async-start | bytes 1048576 | tf_op jit(solution)/shard_map/psum | solution.py:55
  912.9 10.4 copy-start.3
  1205.7 10.8 copy-start.27
  1225.8 88.7 %all-reduce.16.cloned.1.call-start = ((), (), s32[]{:S(2)}) async-start(), calls=%async_computation.12 | async-start | bytes 1048576 | tf_op jit(solution)/shard_map/psum | solution.py:55
  1237.9 35.5 %copy-start.4 = (f32[768,1024]{1,0:T(8,128)S(1)}, f32[768,1024]{1,0:T(8,128)}, u32[]{:S(2)}) copy-start(f32[768,1024]{1,0:T(8,128)} %all-gather.22.cloned.1.call-done) | copy-start | bytes 9437188
  1276.0 89.3 %all-reduce.18.cloned.1.call-start = ((), (), s32[]{:S(2)}) async-start(), calls=%async_computation.13 | async-start | bytes 1048576 | tf_op jit(solution)/shard_map/psum | solution.py:55
  1314.5 9.1 copy-start.15
  1326.8 93.2 %all-reduce.20.cloned.1.call-start = ((), (), s32[]{:S(2)}) async-start(), calls=%async_computation.14 | async-start | bytes 1048576 | tf_op jit(solution)/shard_map/psum | solution.py:55
  1337.9 32.9 %copy-start.16 = (f32[1280,4,32]{0,2,1:T(8,128)S(1)}, f32[1280,4,32]{0,2,1:T(8,128)}, u32[]{:S(2)}) copy-start(f32[1280,4,32]{0,2,1:T(8,128)} %slice.264) | copy-start | bytes 1966084
  1337.9 32.9 %copy-start.19 = (f32[768,128]{0,1:T(8,128)S(1)}, f32[768,128]{0,1:T(8,128)}, u32[]{:S(2)}) copy-start(f32[768,128]{0,1:T(8,128)} %copy-done.18) | copy-start | bytes 1179652
  1381.7 96.5 %all-reduce.22.cloned.1.call-start = ((), (), s32[]{:S(2)}) async-start(), calls=%async_computation.15 | async-start | bytes 1048576 | tf_op jit(solution)/shard_map/psum | solution.py:55
  1381.7 50.8 %copy-start.20 = (f32[768,4,32]{0,2,1:T(8,128)}, f32[768,4,32]{0,2,1:T(8,128)S(1)}, u32[]{:S(2)}) copy-start(f32[768,4,32]{0,2,1:T(8,128)S(1)} %slice.262) | copy-start | bytes 1179652
  1439.7 95.0 %all-reduce.24.cloned.1.call-start = ((), (), s32[]{:S(2)}) async-start(), calls=%async_computation.16 | async-start | bytes 1048576 | tf_op jit(solution)/shard_map/psum | solution.py:55
  1450.7 32.9 %copy-start.21 = (f32[768,4,32]{0,2,1:T(8,128)S(1)}, f32[768,4,32]{0,2,1:T(8,128)}, u32[]{:S(2)}) copy-start(f32[768,4,32]{0,2,1:T(8,128)} %copy-done.20) | copy-start | bytes 1179652
  1478.1 13.0 slice-start
  1496.1 100.1 %all-reduce.26.cloned.1.call-start = ((), (), s32[]{:S(2)}) async-start(), calls=%async_computation.17 | async-start | bytes 1048576 | tf_op jit(solution)/shard_map/psum | solution.py:55
  1539.9 9.9 copy-start.23
  (17 other events, 88.1 us)
Sparse Core Ops, SparseCore 0:
  9.2 25.9 all-gather.25
  37.1 55.4 all-gather.11
  94.5 50.8 all-gather.13
  147.2 46.2 all-gather.15
  195.2 41.6 all-gather.17
  238.6 37.0 all-gather.19
  277.6 32.4 all-gather.21
  311.9 27.8 all-gather.23
  349.3 170.8 all-reduce.27
  521.9 35.3 all-gather.29
  559.2 160.7 all-gather.27
  1225.9 38.6 all-reduce.13
  1276.2 38.3 all-reduce.15
  1327.0 38.2 all-reduce.17
  1381.8 38.2 all-reduce.19
  1439.8 38.3 all-reduce.21
  1496.2 38.3 all-reduce.23
  1557.8 38.3 all-reduce.25

commit v2 on v0

v2 whole, which is shorter than its diff:
```python
import functools

import jax
import jax.numpy as jnp
from jax import lax
from jax.experimental import pallas as pl
from jax.experimental.pallas import tpu as pltpu
from jax.sharding import PartitionSpec as P

F32 = jnp.float32
HI = lax.Precision.HIGHEST
MESH = pl.DeviceIdType.MESH
TR = 256


def dot(a, b, ca, cb):
    return lax.dot_general(a, b, (((ca,), (cb,)), ((), ())), precision=HI, preferred_element_type=F32)


def kernel(na, v_ref, tl_ref, zt_ref, out_ref, vbuf, tbuf, xt, vn, tc, gacc, tm, wp, wrs, ybuf, gpart, grs, gbuf,
           lsem, vsend, vrecv, tsend, trecv, fsend, tfsend, zsend, zrecv, osend, orecv,
           wsend, wrecv, ysend, yrecv, gsend, grecv, hsend, hrecv):
    rr = lax.axis_index("row")
    c = lax.axis_index("col")
    rloc = TR * na
    nsteps = 4 * na
    core, cx, cy = c % 2, (c // 2) % 2, c // 4
    mate = c + 1 - 2 * core
    xn = c + 2 - 4 * cx
    yn = c + 4 - 8 * cy
    dg = yn + 2 - 4 * cx
    same = (xn, yn, dg)

    def zpeer(d):
        return lax.rem(rr + d, 4)

    barrier = pltpu.get_barrier_semaphore()
    for p in (mate, xn, yn, dg):
        pl.semaphore_signal(barrier, inc=1, device_id=(rr, p), device_id_type=MESH)
    for d in (1, 2, 3):
        pl.semaphore_signal(barrier, inc=1, device_id=(zpeer(d), c), device_id_type=MESH)
    pl.semaphore_wait(barrier, 7)

    def rows(a):
        return pl.ds(128 * (na - 1 - a) * (na - a), rloc - TR * a)

    def vdst(q, a):
        return vbuf.at[q, rows(a), :]

    def rc(src, dst, ss, rs, dev):
        return pltpu.make_async_remote_copy(src_ref=src, dst_ref=dst, send_sem=ss, recv_sem=rs,
                                            device_id=dev, device_id_type=MESH)

    def vsrc(a):
        return v_ref.at[pl.ds(TR * a, rloc - TR * a), pl.ds(128 * a, 128)]

    def tsrc(a):
        return tl_ref.at[:, pl.ds(128 * a, 128)]

    def locals_(a):
        return (pltpu.make_async_copy(vsrc(a), vdst(c, a), lsem.at[0, a]),
                pltpu.make_async_copy(tsrc(a), tbuf.at[c, a], lsem.at[1, a]))

    def sends(a):
        out = []
        for n, p in enumerate((xn, yn, dg, mate)):
            out.append(rc(tsrc(a), tbuf.at[c, a], tsend.at[a, n], trecv.at[a, c], (rr, p)))
            out.append(rc(vsrc(a), vdst(c, a), vsend.at[a, n], vrecv.at[a, c], (rr, p)))
        return out

    def forwards(a):
        out = []
        for n, q in enumerate(same):
            out.append(rc(tbuf.at[q, a], tbuf.at[q, a], tfsend.at[a, n], trecv.at[a, q], (rr, mate)))
            out.append(rc(vdst(q, a), vdst(q, a), fsend.at[a, n], vrecv.at[a, q], (rr, mate)))
        return out

    def incoming(a, q):
        return (rc(tbuf.at[q, a], tbuf.at[q, a], tsend.at[a, 0], trecv.at[a, q], (rr, mate)),
                rc(vdst(q, a), vdst(q, a), vsend.at[a, 0], vrecv.at[a, q], (rr, mate)))

    def start_group(a):
        for cp in locals_(a):
            cp.start()
        for cp in sends(a):
            cp.start()

    def forward_group(a):
        for n, q in enumerate(same):
            for cp in incoming(a, q):
                cp.wait_recv()
        for cp in forwards(a):
            cp.start()

    def wait_group(a):
        for cp in locals_(a):
            cp.wait()
        for q in (mate, mate + xn - c, mate + yn - c, mate + dg - c):
            for cp in incoming(a, q):
                cp.wait_recv()

    zin = pltpu.make_async_copy(zt_ref.at[:, pl.ds(pl.multiple_of(rr * rloc, rloc), rloc)],
                                xt.at[pl.ds(pl.multiple_of(32 * rr, 32), 32), :], lsem.at[2, 0])
    zin.start()
    zcp = [rc(zt_ref.at[:, pl.ds(pl.multiple_of(zpeer(d) * rloc, rloc), rloc)],
              xt.at[pl.ds(pl.multiple_of(32 * rr, 32), 32), :],
              zsend.at[d - 1], zrecv.at[d - 1], (zpeer(d), c)) for d in (1, 2, 3)]
    for cp in zcp:
        cp.start()
    for a in range(na - 1, max(na - 4, -1), -1):
        start_group(a)

    lane = lax.broadcasted_iota(jnp.int32, (1, 128), 1)
    lo = lane < 64

    def deint(b, tt):
        first, second = [], []
        r = [pltpu.roll(x, 64, axis=1) for x in b]
        left0, right0 = jnp.where(lo, b[0], r[1]), jnp.where(lo, b[2], r[3])
        left1, right1 = jnp.where(lo, r[0], b[1]), jnp.where(lo, r[2], b[3])
        sel = tt == 0
        return jnp.concatenate([jnp.where(sel, left0, left1), jnp.where(sel, right0, right1)], axis=1)

    def prepare(i):
        a = na - 1 - i // 4
        tt = 1 - (i % 4) // 2
        h = 1 - i % 2
        slot = i % 2
        tc[slot] = deint([tbuf[4 * h + n, a] for n in range(4)], tt)
        gacc[...] = jnp.zeros_like(gacc)
        base = 128 * (na - 1 - a) * (na - a)

        def tile(t, _):
            src = pl.multiple_of(base + (t - a) * TR, 128)
            v = deint([vbuf[4 * h + n, pl.ds(src, TR), :] for n in range(4)], tt)
            vn[slot, pl.ds(pl.multiple_of(t * TR, TR), TR), :] = v
            gacc[...] += dot(v, v, 0, 0)
            return 0

        lax.fori_loop(a, na, tile, 0)
        gpart[0:128, :] = gacc[0:128, 128:256]
        gpart[128:192, :] = jnp.where(lo, pltpu.roll(gacc[0:64, 0:128], 64, axis=1), gacc[128:192, 128:256])

    def gcopies():
        return [rc(gpart.at[pl.ds(pl.multiple_of(48 * zpeer(d), 8), 48), :], grs.at[d - 1],
                   gsend.at[d - 1], grecv.at[d - 1], (zpeer(d), c)) for d in (1, 2, 3)]

    def hcopies(slot):
        mine = pl.ds(pl.multiple_of(48 * rr, 8), 48)
        return [rc(gbuf.at[slot, mine, :], gbuf.at[slot, mine, :],
                   hsend.at[d - 1], hrecv.at[d - 1], (zpeer(d), c)) for d in (1, 2, 3)]

    def gsum(slot):
        mine = pl.ds(pl.multiple_of(48 * rr, 8), 48)
        gbuf[slot, mine, :] = (gpart[mine, :] + grs[0]) + (grs[1] + grs[2])

    def form_t(slot):
        tcv = tc[slot]
        lane2 = lax.broadcasted_iota(jnp.int32, (1, 256), 1) // 64
        dm = jnp.concatenate([jnp.where(lane2 == n, tcv, 0.0) for n in range(4)], axis=0)
        pk = gbuf[slot, 128:192, :]
        z64 = jnp.zeros((64, 128), F32)
        z256 = jnp.zeros((64, 256), F32)
        n1 = jnp.concatenate([jnp.concatenate([jnp.where(lo, 0.0, pltpu.roll(pk, 64, axis=1)), z64], axis=1), z256,
                              jnp.concatenate([z64, jnp.where(lo, 0.0, pk)], axis=1), z256], axis=0)
        tm[...] = dm - dot(dm, dot(n1, dm, 1, 0), 1, 0)
        ta, tb = tm[0:128, 0:128], tm[128:256, 128:256]
        tm[0:128, 128:256] = -dot(ta, dot(gbuf[slot, 0:128, :], tb, 1, 0), 1, 0)

    forward_group(na - 1)
    wait_group(na - 1)
    prepare(0)
    for cp in gcopies():
        cp.start()
    for cp in gcopies():
        cp.wait_recv()
    gsum(0)
    for cp in hcopies(0):
        cp.start()
    zin.wait()
    for cp in zcp:
        cp.wait_recv()
    for cp in hcopies(0):
        cp.wait_recv()
    for cp in gcopies() + hcopies(0):
        cp.wait_send()

    def step(i, _):
        a = na - 1 - i // 4
        slot = i % 2
        nslot = 1 - slot
        for sa in range(na - 1, -1, -1):
            @pl.when(i == 4 * (na - 1 - sa))
            def _():
                if sa >= 1:
                    forward_group(sa - 1)
                if sa >= 4 - 1 and sa - 3 <= na - 4:
                    start_group(sa - 3)

        wp[...] = jnp.zeros_like(wp)

        def wtile(t, _):
            o = pl.multiple_of(t * TR, TR)
            wp[...] += dot(xt[:, pl.ds(o, TR)], vn[slot, pl.ds(o, TR), :], 1, 0)
            return 0

        lax.fori_loop(a, na, wtile, 0)
        wcp = [rc(wp.at[pl.ds(pl.multiple_of(32 * zpeer(d), 32), 32), :], wrs.at[d - 1],
                  wsend.at[d - 1], wrecv.at[d - 1], (zpeer(d), c)) for d in (1, 2, 3)]
        for cp in wcp:
            cp.start()

        @pl.when(i < nsteps - 1)
        def _():
            for sa in range(na - 2, -1, -1):
                @pl.when(i == 4 * (na - 1 - sa) - 1)
                def _():
                    wait_group(sa)
            prepare(i + 1)
            for cp in gcopies():
                cp.start()

        form_t(slot)
        mine = pl.ds(pl.multiple_of(32 * rr, 32), 32)
        for cp in wcp:
            cp.wait_recv()
        ybuf[mine, :] = dot((wp[mine, :] + wrs[0]) + (wrs[1] + wrs[2]), tm[...], 1, 1)
        ycp = [rc(ybuf.at[mine, :], ybuf.at[mine, :], ysend.at[d - 1], yrecv.at[d - 1], (zpeer(d), c))
               for d in (1, 2, 3)]
        for cp in ycp:
            cp.start()

        @pl.when(i < nsteps - 1)
        def _():
            for cp in gcopies():
                cp.wait_recv()
            gsum(nslot)
            for cp in hcopies(nslot):
                cp.start()

        for cp in ycp:
            cp.wait_recv()

        def utile(t, _):
            o = pl.multiple_of(t * TR, TR)
            xt[:, pl.ds(o, TR)] = xt[:, pl.ds(o, TR)] - dot(ybuf[...], vn[slot, pl.ds(o, TR), :], 1, 1)
            return 0

        lax.fori_loop(a, na, utile, 0)
        for cp in wcp + ycp:
            cp.wait_send()

        @pl.when(i < nsteps - 1)
        def _():
            for cp in hcopies(nslot):
                cp.wait_recv()
            for cp in gcopies() + hcopies(nslot):
                cp.wait_send()

        return 0

    lax.fori_loop(0, nsteps, step, 0)

    oloc = pltpu.make_async_copy(xt.at[pl.ds(pl.multiple_of(32 * rr, 32), 32), :],
                                 out_ref.at[:, pl.ds(pl.multiple_of(rr * rloc, rloc), rloc)], lsem.at[2, 0])
    oloc.start()
    ocp = [rc(xt.at[pl.ds(pl.multiple_of(32 * zpeer(d), 32), 32), :],
              out_ref.at[:, pl.ds(pl.multiple_of(rr * rloc, rloc), rloc)],
              osend.at[d - 1], orecv.at[d - 1], (zpeer(d), c)) for d in (1, 2, 3)]
    for cp in ocp:
        cp.start()
    for a in range(na - 1, -1, -1):
        for cp in sends(a) + forwards(a):
            cp.wait_send()
    for cp in zcp:
        cp.wait_send()
    oloc.wait()
    for cp in ocp:
        cp.wait()


def solution(mesh):
    def body(v_loc, t_loc, z_loc):
        nt, bw = t_loc.shape[0], t_loc.shape[1]
        na = nt // 2
        rloc = v_loc.shape[0]
        tl = t_loc.transpose(1, 0, 2).reshape(bw, nt * bw)
        zt = z_loc.T
        dma = pltpu.SemaphoreType.DMA
        tot = 128 * na * (na + 1)
        anyspec = pl.BlockSpec(memory_space=pl.ANY)
        out = pl.pallas_call(
            functools.partial(kernel, na),
            out_shape=jax.ShapeDtypeStruct(zt.shape, F32),
            in_specs=[anyspec] * 3,
            out_specs=anyspec,
            scratch_shapes=[
                pltpu.VMEM((8, tot, 128), F32),
                pltpu.VMEM((8, na, 64, 128), F32),
                pltpu.VMEM((128, rloc), F32),
                pltpu.VMEM((2, rloc, 256), F32),
                pltpu.VMEM((2, 64, 256), F32),
                pltpu.VMEM((256, 256), F32),
                pltpu.VMEM((256, 256), F32),
                pltpu.VMEM((128, 256), F32),
                pltpu.VMEM((3, 32, 256), F32),
                pltpu.VMEM((128, 256), F32),
                pltpu.VMEM((192, 128), F32),
                pltpu.VMEM((3, 48, 128), F32),
                pltpu.VMEM((2, 192, 128), F32),
                dma((3, na)),
                dma((na, 4)), dma((na, 8)), dma((na, 4)), dma((na, 8)), dma((na, 3)), dma((na, 3)),
                dma((3,)), dma((3,)), dma((3,)), dma((3,)),
                dma((3,)), dma((3,)), dma((3,)), dma((3,)), dma((3,)), dma((3,)), dma((3,)), dma((3,)),
            ],
            compiler_params=pltpu.CompilerParams(
                collective_id=0, has_side_effects=True, vmem_limit_bytes=60 * 2**20),
        )(v_loc, tl, zt)
        return out.T

    return jax.shard_map(
        body,
        mesh=mesh,
        in_specs=(P("row", "col"), P("col", None, None), P(None, ("row", "col"))),
        out_specs=P(None, ("row", "col")),
        check_vma=False,
    )
```

time: 3870 us -> 528 us (0.14)
  the two profiles are of different devices: /device:TPU:0 before, /device:TPU:12 now
where the time goes in v2:
time: 528 us
  Pallas kernels  523 us (99%)
    pallas_call x1, Pallas kernels, body(): pl.pallas_call(functools.partial(kernel, na), out_shape=jax.ShapeDtypeStr...  523 us

profile of v2, /device:TPU:12, one launch (start us, length us, event | category | flops | bytes accessed | tf_op | source)
XLA Modules:
  0.0 527.5 jit_solution(740718300994048415)
XLA Ops:
  0.0 1.3 copy.4
  1.4 0.9 reshape.3.tl_ref
  2.2 523.0 %shard_map.37 = f32[32,8192]{1,0:T(8,128)} custom-call(f32[2048,1024]{1,0:T(8,128)} %v_ref.1, f32[64,1024]{1,0:T(8,128)} %reshape.3.tl_ref, f32[32,8192]{1,0:T(8,128)} %bitcast.4), custom_call_target="tpu_custom_call" | custom-call | tf_op jit(solution)/shard_map/pallas_call | solution.py:292
  525.3 2.3 copy.6

commit v3 on v2

v3 whole, which is shorter than its diff:
```python
import functools

import jax
import jax.numpy as jnp
from jax import lax
from jax.experimental import pallas as pl
from jax.experimental.pallas import tpu as pltpu
from jax.sharding import PartitionSpec as P

F32 = jnp.float32
HI = lax.Precision.HIGHEST
MESH = pl.DeviceIdType.MESH
TR = 256


def dot(a, b, ca, cb):
    return lax.dot_general(a, b, (((ca,), (cb,)), ((), ())), precision=HI, preferred_element_type=F32)


def kernel(na, v_ref, tl_ref, zt_ref, out_ref, vbuf, tbuf, xt, vn, tc, tm, wp, wrs, ybuf, gpart, grs, gbuf,
           lsem, zlsem, vsend, vrecv, tsend, trecv, fsend, tfsend, zsend, zrecv, osend, orecv,
           wsend, wrecv, ysend, yrecv, gsend, grecv, hsend, hrecv, psend, precv, pfsend):
    rr = lax.axis_index("row")
    c = lax.axis_index("col")
    rloc = TR * na
    nsteps = 2 * na
    core, cx, cy = c % 2, (c // 2) % 2, c // 4
    mate = c + 1 - 2 * core
    xn = c + 2 - 4 * cx
    yn = c + 4 - 8 * cy
    dg = yn + 2 - 4 * cx
    same = (xn, yn, dg)
    others = (mate, mate + xn - c, mate + yn - c, mate + dg - c)

    def zpeer(d):
        return lax.rem(rr + d, 4)

    def r16(r):
        return pl.ds(pl.multiple_of(16 * r, 16), 16)

    barrier = pltpu.get_barrier_semaphore()
    for p in (mate, xn, yn, dg):
        pl.semaphore_signal(barrier, inc=1, device_id=(rr, p), device_id_type=MESH)
    for d in (1, 2, 3):
        pl.semaphore_signal(barrier, inc=1, device_id=(zpeer(d), c), device_id_type=MESH)
    pl.semaphore_wait(barrier, 7)

    def rows(a):
        return pl.ds(128 * (na - 1 - a) * (na - a), rloc - TR * a)

    def vdst(q, a):
        return vbuf.at[q, rows(a), :]

    def rc(src, dst, ss, rs, dev):
        return pltpu.make_async_remote_copy(src_ref=src, dst_ref=dst, send_sem=ss, recv_sem=rs,
                                            device_id=dev, device_id_type=MESH)

    def vsrc(a):
        return v_ref.at[pl.ds(TR * a, rloc - TR * a), pl.ds(128 * a, 128)]

    def tsrc(a):
        return tl_ref.at[:, pl.ds(128 * a, 128)]

    def locals_(a):
        return (pltpu.make_async_copy(vsrc(a), vdst(c, a), lsem.at[0, a]),
                pltpu.make_async_copy(tsrc(a), tbuf.at[c, a], lsem.at[1, a]))

    def sends(a):
        out = []
        for n, p in enumerate((xn, yn, dg, mate)):
            out.append(rc(tsrc(a), tbuf.at[c, a], tsend.at[a, n], trecv.at[a, c], (rr, p)))
            out.append(rc(vsrc(a), vdst(c, a), vsend.at[a, n], vrecv.at[a, c], (rr, p)))
        return out

    def forwards(a):
        out = []
        for n, q in enumerate(same):
            out.append(rc(tbuf.at[q, a], tbuf.at[q, a], tfsend.at[a, n], trecv.at[a, q], (rr, mate)))
            out.append(rc(vdst(q, a), vdst(q, a), fsend.at[a, n], vrecv.at[a, q], (rr, mate)))
        return out

    def incoming(a, q):
        return (rc(tbuf.at[q, a], tbuf.at[q, a], tsend.at[a, 0], trecv.at[a, q], (rr, mate)),
                rc(vdst(q, a), vdst(q, a), vsend.at[a, 0], vrecv.at[a, q], (rr, mate)))

    def start_group(a):
        for cp in locals_(a):
            cp.start()
        for cp in sends(a):
            cp.start()

    def forward_group(a):
        for q in same:
            for cp in incoming(a, q):
                cp.wait_recv()
        for cp in forwards(a):
            cp.start()

    def wait_group(a):
        for cp in locals_(a):
            cp.wait()
        for q in others:
            for cp in incoming(a, q):
                cp.wait_recv()

    def mycols():
        return pl.ds(pl.multiple_of(rr * rloc, rloc), rloc)

    zin = [pltpu.make_async_copy(zt_ref.at[pl.ds(16 * p, 16), mycols()], xt.at[p, r16(rr), :], zlsem.at[p])
           for p in (0, 1)]
    zcp = [rc(zt_ref.at[pl.ds(16 * p, 16), pl.ds(pl.multiple_of(zpeer(d) * rloc, rloc), rloc)],
              xt.at[p, r16(rr), :], zsend.at[p, d - 1], zrecv.at[p, d - 1], (zpeer(d), c))
           for p in (0, 1) for d in (1, 2, 3)]
    start_group(na - 1)
    for cp in zin + zcp:
        cp.start()
    for a in range(na - 2, max(na - 5, -1), -1):
        start_group(a)

    lane = lax.broadcasted_iota(jnp.int32, (1, 128), 1)
    lo = lane < 64

    def deint(b, tt):
        sel = tt == 0
        out = []
        for n in range(0, 8, 2):
            lft = jnp.where(lo, b[n], pltpu.roll(b[n + 1], 64, axis=1))
            rgt = jnp.where(lo, pltpu.roll(b[n], 64, axis=1), b[n + 1])
            out.append(jnp.where(sel, lft, rgt))
        return jnp.concatenate(out, axis=1)

    def prepare(g):
        a = na - 1 - g // 2
        tt = 1 - g % 2
        slot = lax.rem(g, 3)
        tc[g % 2] = deint([tbuf[n, a] for n in range(8)], tt)
        gpart[...] = jnp.zeros_like(gpart)
        base = 128 * (na - 1 - a) * (na - a)

        def tile(t, _):
            src = pl.ds(pl.multiple_of(base + (t - a) * TR, 128), TR)
            v = deint([vbuf[n, src, :] for n in range(8)], tt)
            vn[slot, pl.ds(pl.multiple_of(t * TR, TR), TR), :] = v
            own = vbuf[c, src, :]
            own = jnp.where(tt == 0, own, pltpu.roll(own, 64, axis=1))[:, 0:64]
            gpart[...] += dot(own, v, 0, 0)
            return 0

        lax.fori_loop(a, na, tile, 0)

    def gcopies():
        return [rc(gpart.at[r16(zpeer(d)), :], grs.at[d - 1],
                   gsend.at[d - 1], grecv.at[d - 1], (zpeer(d), c)) for d in (1, 2, 3)]

    def gmine():
        return pl.ds(pl.multiple_of(64 * c + 16 * rr, 16), 16)

    def slab(q):
        return pl.ds(pl.multiple_of(64 * q, 64), 64)

    def hcopies(gs):
        return [rc(gbuf.at[gs, gmine(), :], gbuf.at[gs, gmine(), :],
                   hsend.at[d - 1], hrecv.at[d - 1], (zpeer(d), c)) for d in (1, 2, 3)]

    def pcopies(gs):
        return [rc(gbuf.at[gs, slab(c), :], gbuf.at[gs, slab(c), :], psend.at[n], precv.at[gs, c], (rr, p))
                for n, p in enumerate((xn, yn, dg, mate))]

    def pforwards(gs):
        return [rc(gbuf.at[gs, slab(q), :], gbuf.at[gs, slab(q), :], pfsend.at[n], precv.at[gs, q], (rr, mate))
                for n, q in enumerate(same)]

    def pin(gs, q):
        return rc(gbuf.at[gs, slab(q), :], gbuf.at[gs, slab(q), :], psend.at[0], precv.at[gs, q], (rr, mate))

    def gram_start():
        for cp in gcopies():
            cp.start()

    def gram_sum(gs):
        for cp in gcopies():
            cp.wait_recv()
        gbuf[gs, gmine(), :] = (gpart[r16(rr), :] + grs[0]) + (grs[1] + grs[2])
        for cp in hcopies(gs):
            cp.start()
        for cp in gcopies():
            cp.wait_send()

    def gram_plane(gs):
        for cp in hcopies(gs):
            cp.wait()
        for cp in pcopies(gs):
            cp.start()

    def gram_forward(gs):
        for q in same:
            pin(gs, q).wait_recv()
        for cp in pforwards(gs):
            cp.start()

    def gram_finish(gs):
        for q in others:
            pin(gs, q).wait_recv()
        for cp in pcopies(gs) + pforwards(gs):
            cp.wait_send()

    lane2 = lax.broadcasted_iota(jnp.int32, (1, 256), 1) // 64

    def form_t(gs):
        z256 = jnp.zeros((64, 256), F32)
        halves = []
        for o in (0, 256):
            tcv = tc[gs, :, o:o + 256]
            dm = jnp.concatenate([jnp.where(lane2 == n, tcv, 0.0) for n in range(4)], axis=0)
            n1 = jnp.concatenate([jnp.where(lane2 == 1, gbuf[gs, o:o + 64, o:o + 256], 0.0), z256,
                                  jnp.where(lane2 == 3, gbuf[gs, o + 128:o + 192, o:o + 256], 0.0), z256], axis=0)
            t1 = dm - dot(dm, dot(n1, dm, 1, 0), 1, 0)
            ta, tb = t1[0:128, 0:128], t1[128:256, 128:256]
            tx = -dot(ta, dot(gbuf[gs, o:o + 128, o + 128:o + 256], tb, 1, 0), 1, 0)
            top = jnp.concatenate([ta, tx], axis=1)
            bot = jnp.concatenate([jnp.zeros((128, 128), F32), tb], axis=1)
            halves.append(jnp.concatenate([top, bot], axis=0))
        tm[gs, 0] = halves[0].T
        tm[gs, 2] = halves[1].T
        tx = dot(halves[0], dot(gbuf[gs, 0:256, 256:512], halves[1], 1, 0), 1, 0)
        tm[gs, 1] = -(tx.T)

    def wcopies(p):
        return [rc(wp.at[p, r16(zpeer(d)), :], wrs.at[p, d - 1],
                   wsend.at[p, d - 1], wrecv.at[p, d - 1], (zpeer(d), c)) for d in (1, 2, 3)]

    def ycopies(p):
        return [rc(ybuf.at[p, r16(rr), :], ybuf.at[p, r16(rr), :],
                   ysend.at[p, d - 1], yrecv.at[p, d - 1], (zpeer(d), c)) for d in (1, 2, 3)]

    def w_part(i, p):
        a = na - 1 - i // 2
        slot = lax.rem(i, 3)
        wp[p] = jnp.zeros((64, 512), F32)

        def wtile(t, _):
            o = pl.ds(pl.multiple_of(t * TR, TR), TR)
            wp[p] += dot(xt[p, :, o], vn[slot, o, :], 1, 0)
            return 0

        lax.fori_loop(a, na, wtile, 0)
        for cp in wcopies(p):
            cp.start()

    def y_part(i, p):
        for cp in wcopies(p):
            cp.wait_recv()
        w = (wp[p, r16(rr), :] + wrs[p, 0]) + (wrs[p, 1] + wrs[p, 2])
        ts = i % 2
        wa, wb = w[:, 0:256], w[:, 256:512]
        ybuf[p, r16(rr), 0:256] = dot(wa, tm[ts, 0], 1, 0) + dot(wb, tm[ts, 1], 1, 0)
        ybuf[p, r16(rr), 256:512] = dot(wb, tm[ts, 2], 1, 0)
        for cp in ycopies(p):
            cp.start()
        for cp in wcopies(p):
            cp.wait_send()

    def x_part(i, p):
        a = na - 1 - i // 2
        slot = lax.rem(i, 3)
        for cp in ycopies(p):
            cp.wait_recv()

        def utile(t, _):
            o = pl.ds(pl.multiple_of(t * TR, TR), TR)
            xt[p, :, o] = xt[p, :, o] - dot(ybuf[p], vn[slot, o, :], 1, 1)
            return 0

        lax.fori_loop(a, na, utile, 0)
        for cp in ycopies(p):
            cp.wait_send()

    forward_group(na - 1)
    wait_group(na - 1)
    prepare(0)
    gram_start()
    gram_sum(0)
    gram_plane(0)
    prepare(1)
    gram_start()
    for cp in zin:
        cp.wait()
    for cp in zcp:
        cp.wait_recv()
    gram_forward(0)
    gram_finish(0)
    form_t(0)
    gram_sum(1)
    if na >= 2:
        forward_group(na - 2)
    if na >= 5:
        start_group(na - 5)

    def step(i, _):
        for sa in range(na - 3, -1, -1):
            @pl.when(i == 2 * (na - 1 - sa) - 3)
            def _():
                forward_group(sa)
                if sa >= 3:
                    start_group(sa - 3)

        ns = (i + 1) % 2
        w_part(i, 0)

        @pl.when(i < nsteps - 1)
        def _():
            gram_plane(ns)

        @pl.when(i > 0)
        def _():
            x_part(i - 1, 1)

        w_part(i, 1)
        y_part(i, 0)

        @pl.when(i < nsteps - 1)
        def _():
            gram_forward(ns)

        for sa in range(na - 2, -1, -1):
            @pl.when(i == 2 * (na - 1 - sa) - 2)
            def _():
                wait_group(sa)

        @pl.when(i < nsteps - 2)
        def _():
            prepare(i + 2)
            gram_start()

        y_part(i, 1)

        @pl.when(i < nsteps - 1)
        def _():
            gram_finish(ns)
            form_t(ns)

        x_part(i, 0)

        @pl.when(i < nsteps - 2)
        def _():
            gram_sum(i % 2)

        return 0

    lax.fori_loop(0, nsteps, step, 0)

    def outcopies(p):
        return [rc(xt.at[p, r16(zpeer(d)), :], out_ref.at[pl.ds(16 * p, 16), mycols()],
                   osend.at[p, d - 1], orecv.at[p, d - 1], (zpeer(d), c)) for d in (1, 2, 3)]

    oloc = [pltpu.make_async_copy(xt.at[p, r16(rr), :], out_ref.at[pl.ds(16 * p, 16), mycols()], zlsem.at[p])
            for p in (0, 1)]
    oloc[0].start()
    for cp in outcopies(0):
        cp.start()
    x_part(nsteps - 1, 1)
    oloc[1].start()
    for cp in outcopies(1):
        cp.start()
    for a in range(na - 1, -1, -1):
        for cp in sends(a) + forwards(a):
            cp.wait_send()
    for cp in zcp:
        cp.wait_send()
    for p in (0, 1):
        oloc[p].wait()
        for cp in outcopies(p):
            cp.wait()


def solution(mesh):
    def body(v_loc, t_loc, z_loc):
        nt, bw = t_loc.shape[0], t_loc.shape[1]
        na = nt // 2
        rloc = v_loc.shape[0]
        tl = t_loc.transpose(1, 0, 2).reshape(bw, nt * bw)
        zt = z_loc.T
        dma = pltpu.SemaphoreType.DMA
        tot = 128 * na * (na + 1)
        anyspec = pl.BlockSpec(memory_space=pl.ANY)
        out = pl.pallas_call(
            functools.partial(kernel, na),
            out_shape=jax.ShapeDtypeStruct(zt.shape, F32),
            in_specs=[anyspec] * 3,
            out_specs=anyspec,
            scratch_shapes=[
                pltpu.VMEM((8, tot, 128), F32),
                pltpu.VMEM((8, na, 64, 128), F32),
                pltpu.VMEM((2, 64, rloc), F32),
                pltpu.VMEM((3, rloc, 512), F32),
                pltpu.VMEM((2, 64, 512), F32),
                pltpu.VMEM((2, 3, 256, 256), F32),
                pltpu.VMEM((2, 64, 512), F32),
                pltpu.VMEM((2, 3, 16, 512), F32),
                pltpu.VMEM((2, 64, 512), F32),
                pltpu.VMEM((64, 512), F32),
                pltpu.VMEM((3, 16, 512), F32),
                pltpu.VMEM((2, 512, 512), F32),
                dma((2, na)), dma((2,)),
                dma((na, 4)), dma((na, 8)), dma((na, 4)), dma((na, 8)), dma((na, 3)), dma((na, 3)),
                dma((2, 3)), dma((2, 3)), dma((2, 3)), dma((2, 3)),
                dma((2, 3)), dma((2, 3)), dma((2, 3)), dma((2, 3)),
                dma((3,)), dma((3,)), dma((3,)), dma((3,)), dma((4,)), dma((2, 8)), dma((3,)),
            ],
            compiler_params=pltpu.CompilerParams(
                collective_id=0, has_side_effects=True, vmem_limit_bytes=67043328),
        )(v_loc, tl, zt)
        return out.T

    return jax.shard_map(
        body,
        mesh=mesh,
        in_specs=(P("row", "col"), P("col", None, None), P(None, ("row", "col"))),
        out_specs=P(None, ("row", "col")),
        check_vma=False,
    )
```

time: 528 us -> 596 us (1.13)
  the two profiles are of different devices: /device:TPU:12 before, /device:TPU:0 now
where the time goes in v3:
time: 596 us
  Pallas kernels  592 us (99%)
    pallas_call x1, Pallas kernels, body(): pl.pallas_call(functools.partial(kernel, na), out_shape=jax.ShapeDtypeStr...  592 us

profile of v3, /device:TPU:0, one launch (start us, length us, event | category | flops | bytes accessed | tf_op | source)
XLA Modules:
  0.0 596.1 jit_solution(8227853592843596746)
XLA Ops:
  0.0 1.3 copy.4
  1.4 0.9 reshape.3.tl_ref
  2.2 591.6 %shard_map.37 = f32[32,8192]{1,0:T(8,128)} custom-call(f32[2048,1024]{1,0:T(8,128)} %v_ref.1, f32[64,1024]{1,0:T(8,128)} %reshape.3.tl_ref, f32[32,8192]{1,0:T(8,128)} %bitcast.4), custom_call_target="tpu_custom_call" | custom-call | tf_op jit(solution)/shard_map/pallas_call | solution.py:386
  593.8 2.3 copy.6

commit v4 on v3

--- a/solution.py
+++ b/solution.py
@@ -17,8 +17,8 @@
     return lax.dot_general(a, b, (((ca,), (cb,)), ((), ())), precision=HI, preferred_element_type=F32)
 
 
-def kernel(na, v_ref, tl_ref, zt_ref, out_ref, vbuf, tbuf, xt, vn, tc, tm, wp, wrs, ybuf, gpart, grs, gbuf,
-           lsem, zlsem, vsend, vrecv, tsend, trecv, fsend, tfsend, zsend, zrecv, osend, orecv,
+def kernel(na, v_ref, tl_ref, zt_ref, out_ref, vbuf, xt, vn, tc, tm, wp, wrs, ybuf, gpart, grs, gbuf,
+           lsem, zlsem, vsend, vrecv, fsend, rsend, zsend, zrecv, osend, orecv,
            wsend, wrecv, ysend, yrecv, gsend, grecv, hsend, hrecv, psend, precv, pfsend):
     rr = lax.axis_index("row")
     c = lax.axis_index("col")
@@ -45,63 +45,62 @@
         pl.semaphore_signal(barrier, inc=1, device_id=(zpeer(d), c), device_id_type=MESH)
     pl.semaphore_wait(barrier, 7)
 
-    def rows(a):
-        return pl.ds(128 * (na - 1 - a) * (na - a), rloc - TR * a)
-
-    def vdst(q, a):
-        return vbuf.at[q, rows(a), :]
+    first = xn + core * (yn - xn)
+    second = yn + core * (xn - yn)
+
+    def base_of(a):
+        return 128 * (na - 1 - a) * (na - a) + 64 * (na - 1 - a)
+
+    def block(q, a):
+        return vbuf.at[q, pl.ds(base_of(a), rloc - TR * a + 64), :]
 
     def rc(src, dst, ss, rs, dev):
         return pltpu.make_async_remote_copy(src_ref=src, dst_ref=dst, send_sem=ss, recv_sem=rs,
                                             device_id=dev, device_id_type=MESH)
 
-    def vsrc(a):
-        return v_ref.at[pl.ds(TR * a, rloc - TR * a), pl.ds(128 * a, 128)]
-
-    def tsrc(a):
-        return tl_ref.at[:, pl.ds(128 * a, 128)]
-
     def locals_(a):
-        return (pltpu.make_async_copy(vsrc(a), vdst(c, a), lsem.at[0, a]),
-                pltpu.make_async_copy(tsrc(a), tbuf.at[c, a], lsem.at[1, a]))
+        n = rloc - TR * a
+        return (pltpu.make_async_copy(tl_ref.at[:, pl.ds(128 * a, 128)],
+                                      vbuf.at[c, pl.ds(base_of(a), 64), :], lsem.at[0, a]),
+                pltpu.make_async_copy(v_ref.at[pl.ds(TR * a, n), pl.ds(128 * a, 128)],
+                                      vbuf.at[c, pl.ds(base_of(a) + 64, n), :], lsem.at[1, a]))
+
+    def move(q, a, sem, p):
+        return rc(block(q, a), block(q, a), sem, vrecv.at[a, q], (rr, p))
 
     def sends(a):
-        out = []
-        for n, p in enumerate((xn, yn, dg, mate)):
-            out.append(rc(tsrc(a), tbuf.at[c, a], tsend.at[a, n], trecv.at[a, c], (rr, p)))
-            out.append(rc(vsrc(a), vdst(c, a), vsend.at[a, n], vrecv.at[a, c], (rr, p)))
-        return out
-
-    def forwards(a):
-        out = []
-        for n, q in enumerate(same):
-            out.append(rc(tbuf.at[q, a], tbuf.at[q, a], tfsend.at[a, n], trecv.at[a, q], (rr, mate)))
-            out.append(rc(vdst(q, a), vdst(q, a), fsend.at[a, n], vrecv.at[a, q], (rr, mate)))
-        return out
-
-    def incoming(a, q):
-        return (rc(tbuf.at[q, a], tbuf.at[q, a], tsend.at[a, 0], trecv.at[a, q], (rr, mate)),
-                rc(vdst(q, a), vdst(q, a), vsend.at[a, 0], vrecv.at[a, q], (rr, mate)))
-
-    def start_group(a):
-        for cp in locals_(a):
-            cp.start()
-        for cp in sends(a):
-            cp.start()
-
-    def forward_group(a):
-        for q in same:
-            for cp in incoming(a, q):
-                cp.wait_recv()
-        for cp in forwards(a):
-            cp.start()
-
-    def wait_group(a):
+        return [move(c, a, vsend.at[a, n], p) for n, p in enumerate((first, second, mate))]
+
+    def near(a):
+        return [move(first, a, rsend.at[a], second), move(first, a, fsend.at[a, 0], mate),
+                move(second, a, fsend.at[a, 1], mate)]
+
+    def far(a):
+        return [move(dg, a, fsend.at[a, 2], mate)]
+
+    def arrive(a, q):
+        move(q, a, vsend.at[a, 0], mate).wait_recv()
+
+    def stage1(a):
         for cp in locals_(a):
             cp.wait()
+        for cp in sends(a):
+            cp.start()
+
+    def stage2(a):
+        arrive(a, first)
+        arrive(a, second)
+        for cp in near(a):
+            cp.start()
+
+    def stage3(a):
+        arrive(a, dg)
+        for cp in far(a):
+            cp.start()
+
+    def stage4(a):
         for q in others:
-            for cp in incoming(a, q):
-                cp.wait_recv()
+            arrive(a, q)
 
     def mycols():
         return pl.ds(pl.multiple_of(rr * rloc, rloc), rloc)
@@ -111,11 +110,14 @@
     zcp = [rc(zt_ref.at[pl.ds(16 * p, 16), pl.ds(pl.multiple_of(zpeer(d) * rloc, rloc), rloc)],
               xt.at[p, r16(rr), :], zsend.at[p, d - 1], zrecv.at[p, d - 1], (zpeer(d), c))
            for p in (0, 1) for d in (1, 2, 3)]
-    start_group(na - 1)
+    for a in range(na - 1, -1, -1):
+        for cp in locals_(a):
+            cp.start()
+    stage1(na - 1)
     for cp in zin + zcp:
         cp.start()
     for a in range(na - 2, max(na - 5, -1), -1):
-        start_group(a)
+        stage1(a)
 
     lane = lax.broadcasted_iota(jnp.int32, (1, 128), 1)
     lo = lane < 64
@@ -133,12 +135,13 @@
         a = na - 1 - g // 2
         tt = 1 - g % 2
         slot = lax.rem(g, 3)
-        tc[g % 2] = deint([tbuf[n, a] for n in range(8)], tt)
+        base = base_of(a)
+        head = pl.ds(pl.multiple_of(base, 64), 64)
+        tc[g % 2] = deint([vbuf[n, head, :] for n in range(8)], tt)
         gpart[...] = jnp.zeros_like(gpart)
-        base = 128 * (na - 1 - a) * (na - a)
 
         def tile(t, _):
-            src = pl.ds(pl.multiple_of(base + (t - a) * TR, 128), TR)
+            src = pl.ds(pl.multiple_of(base + 64 + (t - a) * TR, 64), TR)
             v = deint([vbuf[n, src, :] for n in range(8)], tt)
             vn[slot, pl.ds(pl.multiple_of(t * TR, TR), TR), :] = v
             own = vbuf[c, src, :]
@@ -275,8 +278,9 @@
         for cp in ycopies(p):
             cp.wait_send()
 
-    forward_group(na - 1)
-    wait_group(na - 1)
+    stage2(na - 1)
+    stage3(na - 1)
+    stage4(na - 1)
     prepare(0)
     gram_start()
     gram_sum(0)
@@ -292,24 +296,32 @@
     form_t(0)
     gram_sum(1)
     if na >= 2:
-        forward_group(na - 2)
-    if na >= 5:
-        start_group(na - 5)
+        stage2(na - 2)
+        stage3(na - 2)
 
     def step(i, _):
-        for sa in range(na - 3, -1, -1):
-            @pl.when(i == 2 * (na - 1 - sa) - 3)
-            def _():
-                forward_group(sa)
-                if sa >= 3:
-                    start_group(sa - 3)
-
         ns = (i + 1) % 2
         w_part(i, 0)
 
         @pl.when(i < nsteps - 1)
         def _():
             gram_plane(ns)
+
+        for sa in range(na - 3, -1, -1):
+            due = 2 * (na - 1 - sa) - 2
+
+            @pl.when(i == due - 2)
+            def _():
+                stage2(sa)
+
+            @pl.when(i == due - 1)
+            def _():
+                stage3(sa)
+
+            if due >= 6:
+                @pl.when(i == due - 5)
+                def _():
+                    stage1(sa)
 
         @pl.when(i > 0)
         def _():
@@ -325,7 +337,7 @@
         for sa in range(na - 2, -1, -1):
             @pl.when(i == 2 * (na - 1 - sa) - 2)
             def _():
-                wait_group(sa)
+                stage4(sa)
 
         @pl.when(i < nsteps - 2)
         def _():
@@ -363,7 +375,7 @@
     for cp in outcopies(1):
         cp.start()
     for a in range(na - 1, -1, -1):
-        for cp in sends(a) + forwards(a):
+        for cp in sends(a) + near(a) + far(a):
             cp.wait_send()
     for cp in zcp:
         cp.wait_send()
@@ -381,7 +393,7 @@
         tl = t_loc.transpose(1, 0, 2).reshape(bw, nt * bw)
         zt = z_loc.T
         dma = pltpu.SemaphoreType.DMA
-        tot = 128 * na * (na + 1)
+        tot = 128 * na * (na + 1) + 64 * na
         anyspec = pl.BlockSpec(memory_space=pl.ANY)
         out = pl.pallas_call(
             functools.partial(kernel, na),
@@ -390,7 +402,6 @@
             out_specs=anyspec,
             scratch_shapes=[
                 pltpu.VMEM((8, tot, 128), F32),
-                pltpu.VMEM((8, na, 64, 128), F32),
                 pltpu.VMEM((2, 64, rloc), F32),
                 pltpu.VMEM((3, rloc, 512), F32),
                 pltpu.VMEM((2, 64, 512), F32),
@@ -402,7 +413,7 @@
                 pltpu.VMEM((3, 16, 512), F32),
                 pltpu.VMEM((2, 512, 512), F32),
                 dma((2, na)), dma((2,)),
-                dma((na, 4)), dma((na, 8)), dma((na, 4)), dma((na, 8)), dma((na, 3)), dma((na, 3)),
+                dma((na, 3)), dma((na, 8)), dma((na, 3)), dma((na,)),
                 dma((2, 3)), dma((2, 3)), dma((2, 3)), dma((2, 3)),
                 dma((2, 3)), dma((2, 3)), dma((2, 3)), dma((2, 3)),
                 dma((3,)), dma((3,)), dma((3,)), dma((3,)), dma((4,)), dma((2, 8)), dma((3,)),

time: 596 us -> 479 us (0.80)
  Pallas kernels: 592 us -> 474 us
    pallas_call x1, Pallas kernels: 592 us -> 474 us  [body(): pl.pallas_call(functools.partial(kernel, na), out_shape=jax.ShapeDtypeStr...]
where the time goes in v4:
time: 479 us
  Pallas kernels  474 us (99%)
    pallas_call x1, Pallas kernels, body(): pl.pallas_call(functools.partial(kernel, na), out_shape=jax.ShapeDtypeStr...  474 us

profile of v4, /device:TPU:0, one launch (start us, length us, event | category | flops | bytes accessed | tf_op | source)
XLA Modules:
  0.0 478.6 jit_solution(8473664861675992704)
XLA Ops:
  0.0 1.3 copy.4
  1.4 0.9 reshape.3.tl_ref
  2.2 474.1 %shard_map.37 = f32[32,8192]{1,0:T(8,128)} custom-call(f32[2048,1024]{1,0:T(8,128)} %v_ref.1, f32[64,1024]{1,0:T(8,128)} %reshape.3.tl_ref, f32[32,8192]{1,0:T(8,128)} %bitcast.4), custom_call_target="tpu_custom_call" | custom-call | tf_op jit(solution)/shard_map/pallas_call | solution.py:398
  476.4 2.3 copy.6

commit v5 on v4

--- a/solution.py
+++ b/solution.py
@@ -8,6 +8,7 @@
 from jax.sharding import PartitionSpec as P
 
 F32 = jnp.float32
+BF16 = jnp.bfloat16
 HI = lax.Precision.HIGHEST
 MESH = pl.DeviceIdType.MESH
 TR = 256
@@ -17,7 +18,27 @@
     return lax.dot_general(a, b, (((ca,), (cb,)), ((), ())), precision=HI, preferred_element_type=F32)
 
 
-def kernel(na, v_ref, tl_ref, zt_ref, out_ref, vbuf, xt, vn, tc, tm, wp, wrs, ybuf, gpart, grs, gbuf,
+def split3(x):
+    h = x.astype(BF16)
+    r = x - h.astype(F32)
+    m = r.astype(BF16)
+    return h, m, (r - m.astype(F32)).astype(BF16)
+
+
+def stack3(x):
+    return jnp.concatenate(split3(x), axis=0)
+
+
+def dot6(stack, parts, ca, cb):
+    m = stack.shape[0] // 3
+    dims = (((ca,), (cb,)), ((), ()))
+    r1 = lax.dot_general(stack, parts[0], dims, preferred_element_type=F32)
+    r2 = lax.dot_general(stack[0:2 * m], parts[1], dims, preferred_element_type=F32)
+    r3 = lax.dot_general(stack[0:m], parts[2], dims, preferred_element_type=F32)
+    return (((r1[2 * m:] + r3) + r2[m:]) + (r1[m:2 * m] + r2[0:m])) + r1[0:m]
+
+
+def kernel(na, v_ref, tl_ref, zt_ref, out_ref, vbuf, xt, vnh, vnm, vnl, tmh, tmm, tml, th, wp, wrs, ybuf, ystk, gpart, grs, gbuf,
            lsem, zlsem, vsend, vrecv, fsend, rsend, zsend, zrecv, osend, orecv,
            wsend, wrecv, ysend, yrecv, gsend, grecv, hsend, hrecv, psend, precv, pfsend):
     rr = lax.axis_index("row")
@@ -116,8 +137,7 @@
     stage1(na - 1)
     for cp in zin + zcp:
         cp.start()
-    for a in range(na - 2, max(na - 5, -1), -1):
-        stage1(a)
+    stage1(na - 2)
 
     lane = lax.broadcasted_iota(jnp.int32, (1, 128), 1)
     lo = lane < 64
@@ -125,31 +145,35 @@
     def deint(b, tt):
         sel = tt == 0
         out = []
-        for n in range(0, 8, 2):
+        for n in range(0, len(b), 2):
             lft = jnp.where(lo, b[n], pltpu.roll(b[n + 1], 64, axis=1))
             rgt = jnp.where(lo, pltpu.roll(b[n], 64, axis=1), b[n + 1])
             out.append(jnp.where(sel, lft, rgt))
         return jnp.concatenate(out, axis=1)
+
+    def vrows(slot, t):
+        return pl.ds(pl.multiple_of(slot * rloc - TR * ((slot + 1) // 2) + t * TR, TR), TR)
 
     def prepare(g):
         a = na - 1 - g // 2
         tt = 1 - g % 2
         slot = lax.rem(g, 3)
         base = base_of(a)
-        head = pl.ds(pl.multiple_of(base, 64), 64)
-        tc[g % 2] = deint([vbuf[n, head, :] for n in range(8)], tt)
         gpart[...] = jnp.zeros_like(gpart)
 
-        def tile(t, _):
+        def tile(k, _):
+            t, hb = k // 2, k % 2
             src = pl.ds(pl.multiple_of(base + 64 + (t - a) * TR, 64), TR)
-            v = deint([vbuf[n, src, :] for n in range(8)], tt)
-            vn[slot, pl.ds(pl.multiple_of(t * TR, TR), TR), :] = v
+            v3 = split3(deint([vbuf[4 * hb + n, src, :] for n in range(4)], tt))
+            o = vrows(slot, t)
+            cols = pl.ds(pl.multiple_of(256 * hb, 256), 256)
+            vnh[o, cols], vnm[o, cols], vnl[o, cols] = v3
             own = vbuf[c, src, :]
-            own = jnp.where(tt == 0, own, pltpu.roll(own, 64, axis=1))[:, 0:64]
-            gpart[...] += dot(own, v, 0, 0)
-            return 0
-
-        lax.fori_loop(a, na, tile, 0)
+            own = jnp.where(tt == 0, own, pltpu.roll(own, 64, axis=1)).T[0:64, :]
+            gpart[:, cols] += dot6(stack3(own), v3, 1, 0)
+            return 0
+
+        lax.fori_loop(2 * a, 2 * na, tile, 0)
 
     def gcopies():
         return [rc(gpart.at[r16(zpeer(d)), :], grs.at[d - 1],
@@ -209,24 +233,60 @@
 
     lane2 = lax.broadcasted_iota(jnp.int32, (1, 256), 1) // 64
 
-    def form_t(gs):
+    def form_t(g_idx):
+        gs = g_idx % 2
+        ga = na - 1 - g_idx // 2
+        gt = 1 - g_idx % 2
+        head = pl.ds(pl.multiple_of(base_of(ga), 64), 64)
         z256 = jnp.zeros((64, 256), F32)
-        halves = []
-        for o in (0, 256):
-            tcv = tc[gs, :, o:o + 256]
-            dm = jnp.concatenate([jnp.where(lane2 == n, tcv, 0.0) for n in range(4)], axis=0)
-            n1 = jnp.concatenate([jnp.where(lane2 == 1, gbuf[gs, o:o + 64, o:o + 256], 0.0), z256,
-                                  jnp.where(lane2 == 3, gbuf[gs, o + 128:o + 192, o:o + 256], 0.0), z256], axis=0)
-            t1 = dm - dot(dm, dot(n1, dm, 1, 0), 1, 0)
-            ta, tb = t1[0:128, 0:128], t1[128:256, 128:256]
-            tx = -dot(ta, dot(gbuf[gs, o:o + 128, o + 128:o + 256], tb, 1, 0), 1, 0)
-            top = jnp.concatenate([ta, tx], axis=1)
-            bot = jnp.concatenate([jnp.zeros((128, 128), F32), tb], axis=1)
-            halves.append(jnp.concatenate([top, bot], axis=0))
-        tm[gs, 0] = halves[0].T
-        tm[gs, 2] = halves[1].T
-        tx = dot(halves[0], dot(gbuf[gs, 0:256, 256:512], halves[1], 1, 0), 1, 0)
-        tm[gs, 1] = -(tx.T)
+
+        def half(n, _):
+            o = pl.ds(pl.multiple_of(256 * n, 256), 256)
+            tcv = deint([vbuf[4 * n + k, head, :] for k in range(4)], gt)
+            th[n] = jnp.concatenate([jnp.where(lane2 == k, tcv, 0.0) for k in range(4)], axis=0)
+            g = gbuf.at[gs, o, o]
+            th[3] = jnp.concatenate([jnp.where(lane2 == 1, g[0:64, :], 0.0), z256,
+                                     jnp.where(lane2 == 3, g[128:192, :], 0.0), z256], axis=0)
+
+            def na_(k, _):
+                q = pl.ds(pl.multiple_of(64 * k, 64), 64)
+                th[2, q, :] = dot6(stack3(th[3, q, :]), split3(th[n]), 1, 0)
+                return 0
+
+            lax.fori_loop(0, 4, na_, 0)
+
+            def nb_(k, _):
+                q = pl.ds(pl.multiple_of(64 * k, 64), 64)
+                th[n, q, :] = th[n, q, :] - dot6(stack3(th[n, q, :]), split3(th[2]), 1, 0)
+                return 0
+
+            lax.fori_loop(0, 4, nb_, 0)
+            tx = dot(g[0:128, 128:256], th[n, 128:256, 128:256], 1, 0)
+            th[n, 0:128, 128:256] = -dot(th[n, 0:128, 0:128], tx, 1, 0)
+            return 0
+
+        lax.fori_loop(0, 2, half, 0)
+
+        def nc_(k, _):
+            q = pl.ds(pl.multiple_of(64 * k, 64), 64)
+            th[2, q, :] = dot6(stack3(gbuf[gs, q, 256:512]), split3(th[1]), 1, 0)
+            return 0
+
+        lax.fori_loop(0, 4, nc_, 0)
+
+        def nd_(k, _):
+            q = pl.ds(pl.multiple_of(64 * k, 64), 64)
+            th[3, q, :] = -dot6(stack3(th[0, q, :]), split3(th[2]), 1, 0)
+            return 0
+
+        lax.fori_loop(0, 4, nd_, 0)
+
+        def put(n, _):
+            src = lax.rem(3 * n, 5)
+            tmh[gs, n], tmm[gs, n], tml[gs, n] = split3(th[src].T)
+            return 0
+
+        lax.fori_loop(0, 3, put, 0)
 
     def wcopies(p):
         return [rc(wp.at[p, r16(zpeer(d)), :], wrs.at[p, d - 1],
@@ -243,7 +303,10 @@
 
         def wtile(t, _):
             o = pl.ds(pl.multiple_of(t * TR, TR), TR)
-            wp[p] += dot(xt[p, :, o], vn[slot, o, :], 1, 0)
+            vo = vrows(slot, t)
+            x3 = stack3(xt[p, :, o])
+            for h in (slice(0, 256), slice(256, 512)):
+                wp[p, :, h] += dot6(x3, (vnh[vo, h], vnm[vo, h], vnl[vo, h]), 1, 0)
             return 0
 
         lax.fori_loop(a, na, wtile, 0)
@@ -255,9 +318,10 @@
             cp.wait_recv()
         w = (wp[p, r16(rr), :] + wrs[p, 0]) + (wrs[p, 1] + wrs[p, 2])
         ts = i % 2
-        wa, wb = w[:, 0:256], w[:, 256:512]
-        ybuf[p, r16(rr), 0:256] = dot(wa, tm[ts, 0], 1, 0) + dot(wb, tm[ts, 1], 1, 0)
-        ybuf[p, r16(rr), 256:512] = dot(wb, tm[ts, 2], 1, 0)
+        wa, wb = stack3(w[:, 0:256]), stack3(w[:, 256:512])
+        tb = [(tmh[ts, n], tmm[ts, n], tml[ts, n]) for n in range(3)]
+        ybuf[p, r16(rr), 0:256] = dot6(wa, tb[0], 1, 0) + dot6(wb, tb[1], 1, 0)
+        ybuf[p, r16(rr), 256:512] = dot6(wb, tb[2], 1, 0)
         for cp in ycopies(p):
             cp.start()
         for cp in wcopies(p):
@@ -268,10 +332,12 @@
         slot = lax.rem(i, 3)
         for cp in ycopies(p):
             cp.wait_recv()
+        ystk[...] = stack3(ybuf[p])
 
         def utile(t, _):
             o = pl.ds(pl.multiple_of(t * TR, TR), TR)
-            xt[p, :, o] = xt[p, :, o] - dot(ybuf[p], vn[slot, o, :], 1, 1)
+            vo = vrows(slot, t)
+            xt[p, :, o] = xt[p, :, o] - dot6(ystk[...], (vnh[vo, :], vnm[vo, :], vnl[vo, :]), 1, 1)
             return 0
 
         lax.fori_loop(a, na, utile, 0)
@@ -285,6 +351,8 @@
     gram_start()
     gram_sum(0)
     gram_plane(0)
+    if na >= 3:
+        stage1(na - 3)
     prepare(1)
     gram_start()
     for cp in zin:
@@ -318,8 +386,8 @@
             def _():
                 stage3(sa)
 
-            if due >= 6:
-                @pl.when(i == due - 5)
+            if due >= 4:
+                @pl.when(i == max(due - 5, 0))
                 def _():
                     stage1(sa)
 
@@ -349,7 +417,7 @@
         @pl.when(i < nsteps - 1)
         def _():
             gram_finish(ns)
-            form_t(ns)
+            form_t(i + 1)
 
         x_part(i, 0)
 
@@ -403,12 +471,13 @@
             scratch_shapes=[
                 pltpu.VMEM((8, tot, 128), F32),
                 pltpu.VMEM((2, 64, rloc), F32),
-                pltpu.VMEM((3, rloc, 512), F32),
-                pltpu.VMEM((2, 64, 512), F32),
-                pltpu.VMEM((2, 3, 256, 256), F32),
+                pltpu.VMEM((3 * rloc - TR, 512), BF16), pltpu.VMEM((3 * rloc - TR, 512), BF16), pltpu.VMEM((3 * rloc - TR, 512), BF16),
+                pltpu.VMEM((2, 3, 256, 256), BF16), pltpu.VMEM((2, 3, 256, 256), BF16), pltpu.VMEM((2, 3, 256, 256), BF16),
+                pltpu.VMEM((4, 256, 256), F32),
                 pltpu.VMEM((2, 64, 512), F32),
                 pltpu.VMEM((2, 3, 16, 512), F32),
                 pltpu.VMEM((2, 64, 512), F32),
+                pltpu.VMEM((192, 512), BF16),
                 pltpu.VMEM((64, 512), F32),
                 pltpu.VMEM((3, 16, 512), F32),
                 pltpu.VMEM((2, 512, 512), F32),

time: 479 us -> 488 us (1.019)
  Pallas kernels: 474 us -> 482 us
    pallas_call x1, Pallas kernels: 474 us -> 482 us  [body(): pl.pallas_call(functools.partial(kernel, na), out_shape=jax.ShapeDtypeStr...]
where the time goes in v5:
time: 488 us; the launch traced here: 487 us
  Pallas kernels  482 us (99%)
    pallas_call x1, Pallas kernels, body(): pl.pallas_call(functools.partial(kernel, na), out_shape=jax.ShapeDtypeStr...  482 us

profile of v5, /device:TPU:0, one launch (start us, length us, event | category | flops | bytes accessed | tf_op | source)
XLA Modules:
  0.0 487.0 jit_solution(2087868679293623374)
XLA Ops:
  0.0 1.3 copy.4
  1.4 0.9 reshape.3.tl_ref
  2.2 482.5 %shard_map.37 = f32[32,8192]{1,0:T(8,128)} custom-call(f32[2048,1024]{1,0:T(8,128)} %v_ref.1, f32[64,1024]{1,0:T(8,128)} %reshape.3.tl_ref, f32[32,8192]{1,0:T(8,128)} %bitcast.4), custom_call_target="tpu_custom_call" | custom-call | tf_op jit(solution)/shard_map/pallas_call | solution.py:466
  484.7 2.3 copy.6

commit v6 on v5

--- a/solution.py
+++ b/solution.py
@@ -351,8 +351,8 @@
     gram_start()
     gram_sum(0)
     gram_plane(0)
-    if na >= 3:
-        stage1(na - 3)
+    for a in range(na - 3, max(na - 5, -1), -1):
+        stage1(a)
     prepare(1)
     gram_start()
     for cp in zin:
@@ -375,6 +375,17 @@
         def _():
             gram_plane(ns)
 
+        @pl.when(i > 0)
+        def _():
+            x_part(i - 1, 1)
+
+        w_part(i, 1)
+        y_part(i, 0)
+
+        @pl.when(i < nsteps - 1)
+        def _():
+            gram_forward(ns)
+
         for sa in range(na - 3, -1, -1):
             due = 2 * (na - 1 - sa) - 2
 
@@ -386,21 +397,10 @@
             def _():
                 stage3(sa)
 
-            if due >= 4:
-                @pl.when(i == max(due - 5, 0))
+            if due >= 6:
+                @pl.when(i == due - 6)
                 def _():
                     stage1(sa)
-
-        @pl.when(i > 0)
-        def _():
-            x_part(i - 1, 1)
-
-        w_part(i, 1)
-        y_part(i, 0)
-
-        @pl.when(i < nsteps - 1)
-        def _():
-            gram_forward(ns)
 
         for sa in range(na - 2, -1, -1):
             @pl.when(i == 2 * (na - 1 - sa) - 2)

time: 488 us -> 521 us (1.068)
  Pallas kernels: 482 us -> 516 us
    pallas_call x1, Pallas kernels: 482 us -> 516 us  [body(): pl.pallas_call(functools.partial(kernel, na), out_shape=jax.ShapeDtypeStr...]
where the time goes in v6:
time: 521 us
  Pallas kernels  516 us (99%)
    pallas_call x1, Pallas kernels, body(): pl.pallas_call(functools.partial(kernel, na), out_shape=jax.ShapeDtypeStr...  516 us

profile of v6, /device:TPU:0, one launch (start us, length us, event | category | flops | bytes accessed | tf_op | source)
XLA Modules:
  0.0 520.5 jit_solution(995891826240114755)
XLA Ops:
  0.0 1.3 copy.4
  1.4 0.9 reshape.3.tl_ref
  2.2 516.0 %shard_map.37 = f32[32,8192]{1,0:T(8,128)} custom-call(f32[2048,1024]{1,0:T(8,128)} %v_ref.1, f32[64,1024]{1,0:T(8,128)} %reshape.3.tl_ref, f32[32,8192]{1,0:T(8,128)} %bitcast.4), custom_call_target="tpu_custom_call" | custom-call | tf_op jit(solution)/shard_map/pallas_call | solution.py:466
  518.3 2.3 copy.6
